TPU v7x, 128 devices: a whole 4x4x4 slice. The times are simulated.
128 devices in a mesh: dp: 32 (over z, y_hi, x), expert: 4 (over y_lo, core).
Axes of the slice: x: 4, y: 4 (y_hi: 2, y_lo: 2; y = y_hi * 2 + y_lo), z: 4, core: 2. Of those that a mesh axis runs over, the one named last changes fastest.
Arguments:
- acts: bfloat16 [4, 16384, 4096], P('expert', 'dp'), may hold values from -8 to 8
- cotangent: bfloat16 [4, 16384, 14336], P('expert', 'dp'), may hold values from -1 to 1
- basis: bfloat16 [4, 4096, 256], P('expert'), may hold values from -1 to 1, as said below
- first_moment: float32 [4, 256, 14336], P('expert', 'dp'), may hold values from -0.6 to 0.6
- second_moment: float32 [4, 256, 14336], P('expert', 'dp'), may hold values from 0.001 to 0.05
- step_count: int32 [1], replicated, may hold values from 1 to 20
Outputs:
- update: bfloat16 [4, 4096, 14336], P('expert', 'dp')
- new_first: float32 [4, 256, 14336], P('expert', 'dp')
- new_second: float32 [4, 256, 14336], P('expert', 'dp')
Inputs may be any that keep to these rules, and one draw needn't show every extreme that they name: Each expert's basis has orthonormal columns.
All inputs are finite; a program needn't handle non-finite values.
Results may differ from a plain program's by a relative error of at most 0.0051.
Values may be sent and summed in bfloat16 or wider, within the bound.
A program may use at most 128 MiB of HBM per device.

v0:
```python
import jax
import jax.numpy as jnp
from jax import lax
from jax.sharding import Mesh
from jax.sharding import PartitionSpec as P

D = 4096
FF = 14336
R = 256
DP = ("dp_0", "dp_1", "dp_2")
DP_EXPERT = ("dp_0", "dp_1", "dp_2", "expert_0", "expert_1")
EXPERT = ("expert_0", "expert_1")


def reduced_to_own(blocks, axes, sequence):
    inside = blocks.shape[1:]
    blocks = blocks.reshape(*(lax.axis_size(a) for a in axes), *inside)
    blocks = jnp.moveaxis(blocks, sequence, range(len(axes))).reshape(-1, *inside)
    for k in sequence:
        blocks = lax.psum_scatter(blocks, axes[k], scatter_dimension=0, tiled=True)
    return blocks[0]


def cut_along(array, dim, size):
    before, after = (array.shape[:dim], array.shape[dim + 1 :])
    return jnp.moveaxis(array.reshape(*before, size, -1, *after), dim, 0)


def scatter_axes(array, axes, sequence, dim):
    size = lax.axis_size(axes)
    return reduced_to_own(cut_along(array, dim, size), axes, sequence)


def one_axis_at_a_time(array, axes):
    for axis in axes:
        array = lax.psum(array, axis)
    return array


def local(acts, cotangent, basis, first_moment, second_moment, step_count):
    local_experts = acts.shape[0]
    dp_index = lax.axis_index(DP)
    reduced = jnp.einsum("etd,edr->ert", acts, basis, preferred_element_type=jnp.float32).astype(
        jnp.bfloat16
    )
    shared = scatter_axes(
        jnp.einsum("ekt,etf->kef", reduced, cotangent, preferred_element_type=jnp.float32),
        DP,
        (0, 2, 1),
        0,
    )
    sums = jnp.transpose(shared, (1, 0, 2))
    local_total = jnp.sum(sums * sums)
    total = one_axis_at_a_time(local_total, DP_EXPERT)
    all_experts = local_experts * lax.axis_size(EXPERT)
    limit = 0.25 * jnp.sqrt(jnp.float32(all_experts * R * FF))
    factor = jnp.minimum(jnp.float32(1.0), limit / jnp.sqrt(total + 1e-06))
    grad = sums * factor
    new_first = 0.9 * first_moment + 0.1 * grad
    new_second = 0.999 * second_moment + 0.001 * grad * grad
    steps = step_count[0].astype(jnp.float32)
    corr_one = 1.0 - jnp.power(jnp.float32(0.9), steps)
    corr_two = 1.0 - jnp.power(jnp.float32(0.999), steps)
    normed = (new_first / corr_one / (jnp.sqrt(new_second / corr_two) + 1e-08)).astype(jnp.bfloat16)
    width_rows = D // lax.axis_size(DP)
    basis_rows = lax.dynamic_slice_in_dim(basis, dp_index * width_rows, width_rows, 1)
    gathered = lax.all_gather(normed, DP, axis=1, tiled=True)
    product = jnp.einsum("edk,ekf->edf", basis_rows, gathered, preferred_element_type=jnp.float32)
    update = (0.25 * product).astype(jnp.bfloat16)
    return (update, new_first, new_second)


def solution(mesh):
    split = Mesh(
        mesh.devices.reshape(4, 2, 4, 2, 2), ("dp_0", "dp_1", "dp_2", "expert_0", "expert_1")
    )
    return jax.shard_map(
        local,
        mesh=split,
        in_specs=(
            P(EXPERT, DP, None),
            P(EXPERT, DP, None),
            P(EXPERT, None, None),
            P(EXPERT, DP, None),
            P(EXPERT, DP, None),
            P(),
        ),
        out_specs=(P(EXPERT, DP, None), P(EXPERT, DP, None), P(EXPERT, DP, None)),
        check_vma=False,
    )
```

profile of v0, /device:TPU:0, one launch (start us, length us, event | category | flops | bytes accessed | tf_op | source)
XLA Modules:
  0.0 389.1 jit_solution(2449143444567633862)
XLA Ops:
  7.2 0.0 copy-start
  7.2 0.0 reduce-scatter.4.cloned.1.call-start
  7.2 1.5 copy-done
  8.8 3.5 fusion.8
  12.2 12.8 %fusion.2 = f32[256,14336]{1,0:T(8,128)} fusion(bf16[256,512]{1,0:T(8,128)(2,1)S(1)} %fusion.8, bf16[1,512,14336]{2,1,0:T(8,128)(2,1)} %param.7), kind=kOutput, calls=%fused_computation.3 | convolution fusion | flops 3758096384 | bytes 29622272 | tf_op jit(solution)/shard_map/ekt,etf->kef/dot_general | solution.py:47
  25.0 12.0 %copy.9 = f32[4,4,2,8,1,14336]{5,3,2,1,0,4:T(8,128)} copy(f32[4,4,2,8,1,14336]{5,3,1,2,0,4:T(8,128)} %bitcast.42) | data formatting | bytes 29360128 | tf_op jit(solution)/shard_map/transpose | solution.py:18
  37.0 0.0 copy-start.1
  37.0 0.0 copy-start.2
  37.0 0.0 reduce-scatter.4.cloned.1.call-update
  37.0 0.0 reduce-scatter.6.cloned.1.call-start
  37.1 134.3 %reduce-scatter.4.cloned.1.call-done = f32[8,8,1,14336]{3,1,2,0:T(8,128)} async-done(((f32[32,8,1,14336]{3,1,2,0:T(8,128)}), f32[8,8,1,14336]{3,1,2,0:T(8,128)}) %reduce-scatter.4.cloned.1.call-update) | async-done | bytes 3670032 | tf_op jit(solution)/shard_map/reduce_scatter | solution.py:20
  171.4 0.0 reduce-scatter.6.cloned.1.call-update
  171.4 0.0 reduce-scatter.8.cloned.1.call-start
  171.5 44.5 %reduce-scatter.6.cloned.1.call-done = f32[2,8,1,14336]{3,1,2,0:T(8,128)} async-done(((f32[8,8,1,14336]{3,1,2,0:T(8,128)}), f32[2,8,1,14336]{3,1,2,0:T(8,128)}) %reduce-scatter.6.cloned.1.call-update) | async-done | bytes 917520 | tf_op jit(solution)/shard_map/reduce_scatter | solution.py:20
  215.9 0.0 reduce-scatter.8.cloned.1.call-update
  215.9 0.0 all-gather.2.cloned.1.call-start
  216.6 24.4 %reduce-scatter.8.cloned.1.call-done = f32[1,8,1,14336]{3,1,2,0:T(8,128)} async-done(((f32[2,8,1,14336]{3,1,2,0:T(8,128)}), f32[1,8,1,14336]{3,1,2,0:T(8,128)}) %reduce-scatter.8.cloned.1.call-update) | async-done | bytes 458768 | tf_op jit(solution)/shard_map/reduce_scatter | solution.py:20
  241.1 1.7 multiply_reduce_fusion
  242.8 11.3 %psum.35 = f32[]{:T(128)} all-reduce(f32[]{:T(128)} %multiply_reduce_fusion), channel_id=1, replica_groups=mesh['dp_0'=4,'dp_1'=2,'dp_2'=4,'expert_0'=2,'expert_1'=2] {'dp_0'}, use_global_device_ids=true, to_apply=%region_4.0 | all-reduce | flops 1 | bytes 8 | tf_op jit(solution)/shard_map/psum | solution.py:36
  254.1 7.1 %psum.36 = f32[]{:T(128)} all-reduce(f32[]{:T(128)} %psum.35), channel_id=1, replica_groups=mesh['dp_0'=4,'dp_1'=2,'dp_2'=4,'expert_0'=2,'expert_1'=2] {'dp_1'}, use_global_device_ids=true, to_apply=%region_5.0 | all-reduce | flops 1 | bytes 8 | tf_op jit(solution)/shard_map/psum | solution.py:36
  261.3 11.1 %psum.37 = f32[]{:T(128)} all-reduce(f32[]{:T(128)} %psum.36), channel_id=1, replica_groups=mesh['dp_0'=4,'dp_1'=2,'dp_2'=4,'expert_0'=2,'expert_1'=2] {'dp_2'}, use_global_device_ids=true, to_apply=%region_6.0 | all-reduce | flops 1 | bytes 8 | tf_op jit(solution)/shard_map/psum | solution.py:36
  272.3 5.5 %psum.38 = f32[]{:T(128)} all-reduce(f32[]{:T(128)} %psum.37), channel_id=1, replica_groups=mesh['dp_0'=4,'dp_1'=2,'dp_2'=4,'expert_0'=2,'expert_1'=2] {'expert_0'}, use_global_device_ids=true, to_apply=%region_7.0 | all-reduce | flops 1 | bytes 8 | tf_op jit(solution)/shard_map/psum | solution.py:36
  277.9 3.1 psum.39
  281.6 0.0 copy-done.1
  281.7 0.0 copy-done.2
  281.7 2.2 divide_convert_fusion
  283.8 0.0 all-gather.2.cloned.1.call-update
  283.9 92.6 %all-gather.2.cloned.1.call-done = bf16[1,256,14336]{2,1,0:T(8,128)(2,1)} async-done(((bf16[1,8,14336]{2,1,0:T(8,128)(2,1)}), bf16[1,256,14336]{2,1,0:T(8,128)(2,1)}) %all-gather.2.cloned.1.call-update) | async-done | bytes 7340048 | tf_op jit(solution)/shard_map/all_gather | solution.py:67
  376.5 6.1 %fusion.1 = bf16[1,128,14336]{2,1,0:T(8,128)(2,1)} fusion(bf16[1,256,14336]{2,1,0:T(8,128)(2,1)} %all-gather.2.cloned.1.call-done, bf16[1,4096,256]{2,1,0:T(8,128)(2,1)S(1)} %copy-done, s32[]{:T(128)S(6)} %select_n.3), kind=kOutput, calls=%fused_computation.2 | convolution fusion | flops 943194112 | bytes 11075588 | tf_op jit(solution)/shard_map/edk,ekf->edf/dot_general | solution.py:68
Async XLA Ops:
  7.2 1.6 copy-start
  7.2 164.2 %reduce-scatter.4.cloned.1.call-start = ((), (), s32[]{:S(2)}) async-start(), calls=%async_computation.3 | async-start | bytes 18350080 | tf_op jit(solution)/shard_map/reduce_scatter | solution.py:20
  37.0 244.7 %copy-start.1 = (f32[1,8,14336]{2,1,0:T(8,128)S(1)}, f32[1,8,14336]{2,1,0:T(8,128)}, u32[]{:S(2)}) copy-start(f32[1,8,14336]{2,1,0:T(8,128)} %param.10) | copy-start | bytes 1376260
  37.0 244.7 %copy-start.2 = (f32[1,8,14336]{2,1,0:T(8,128)S(1)}, f32[1,8,14336]{2,1,0:T(8,128)}, u32[]{:S(2)}) copy-start(f32[1,8,14336]{2,1,0:T(8,128)} %param.9) | copy-start | bytes 1376260
  37.0 178.9 %reduce-scatter.6.cloned.1.call-start = ((), (), s32[]{:S(2)}) async-start(), calls=%async_computation.4 | async-start | bytes 4587520 | tf_op jit(solution)/shard_map/reduce_scatter | solution.py:20
  171.4 69.6 %reduce-scatter.8.cloned.1.call-start = ((), (), s32[]{:S(2)}) async-start(), calls=%async_computation.5 | async-start | bytes 1376256 | tf_op jit(solution)/shard_map/reduce_scatter | solution.py:20
  215.9 160.5 %all-gather.2.cloned.1.call-start = ((), (), s32[]{:S(2)}) async-start(), calls=%async_computation.6 | async-start | bytes 7569408 | tf_op jit(solution)/shard_map/all_gather | solution.py:67
Sparse Core Ops, SparseCore 0:
  37.1 134.2 reduce-scatter.3
  173.8 42.0 reduce-scatter.5
  218.3 22.7 reduce-scatter.7
  284.0 92.4 all-gather.1
where the time goes:
time: 390 us; the launch traced here: 389 us
  waiting for transfers between devices  296 us (76%)
  blocking collectives  38 us (10%)
  matrix products  22.3 us (6%)
  between operations  15.2 us (4%)
  local copies, waits for them, and re-layouts  13.5 us (3%)
  other arithmetic  3.91 us (1%)
    reduce_scatter x3, waiting for transfers between devices, reduced_to_own(): blocks = lax.psum_scatter(blocks, axes[k], scatter_dimension=0, tiled=True)  203 us
    all_gather x1, waiting for transfers between devices, local(): gathered = lax.all_gather(normed, DP, axis=1, tiled=True)  92.6 us
    psum x5, blocking collectives, one_axis_at_a_time(): array = lax.psum(array, axis)  38 us
    dot_general x1, matrix products, local(): jnp.einsum('ekt,etf->kef', reduced, cotangent, preferred_element_type=jnp...  12.8 us
    transpose x1, local copies, waits for them, and re-layouts, reduced_to_own(): jnp.moveaxis(blocks, sequence, range(len(axes))).reshape(-1, *inside)  12 us
  transfers between devices with their start and end apart: 4, of which 4 were waited for; matrix products, arithmetic and copies ran while one was open for 0% of the time, Pallas kernels for 0%

commit v1 on v0

--- a/solution.py
+++ b/solution.py
@@ -44,14 +44,16 @@
         jnp.bfloat16
     )
     shared = scatter_axes(
-        jnp.einsum("ekt,etf->kef", reduced, cotangent, preferred_element_type=jnp.float32),
+        jnp.einsum("ekt,etf->kef", reduced, cotangent, preferred_element_type=jnp.float32).astype(
+            jnp.bfloat16
+        ),
         DP,
         (0, 2, 1),
         0,
     )
-    sums = jnp.transpose(shared, (1, 0, 2))
+    sums = jnp.transpose(shared, (1, 0, 2)).astype(jnp.float32)
     local_total = jnp.sum(sums * sums)
-    total = one_axis_at_a_time(local_total, DP_EXPERT)
+    total = lax.psum(local_total, DP_EXPERT)
     all_experts = local_experts * lax.axis_size(EXPERT)
     limit = 0.25 * jnp.sqrt(jnp.float32(all_experts * R * FF))
     factor = jnp.minimum(jnp.float32(1.0), limit / jnp.sqrt(total + 1e-06))

time: 390 us -> 328 us (0.84)
  waiting for transfers between devices: 296 us -> 219 us
  blocking collectives: 38 us -> 64.8 us
  local copies, waits for them, and re-layouts: 13.5 us -> 5.28 us
    reduce_scatter x3, waiting for transfers between devices: 203 us -> 124 us  [reduced_to_own(): blocks = lax.psum_scatter(blocks, axes[k], scatter_dimension=0, tiled=True)]
    psum x5 -> x1, blocking collectives: 38 us -> 64.8 us  [local(): total = lax.psum(local_total, DP_EXPERT)]
    transpose x1, local copies, waits for them, and re-layouts: 12 us -> 3.73 us  [reduced_to_own(): jnp.moveaxis(blocks, sequence, range(len(axes))).reshape(-1, *inside)]
where the time goes in v1:
time: 328 us
  waiting for transfers between devices  219 us (67%)
  blocking collectives  64.8 us (20%)
  matrix products  19.4 us (6%)
  between operations  15.2 us (5%)
  local copies, waits for them, and re-layouts  5.28 us (2%)
  other arithmetic  3.76 us (1%)
    reduce_scatter x3, waiting for transfers between devices, reduced_to_own(): blocks = lax.psum_scatter(blocks, axes[k], scatter_dimension=0, tiled=True)  124 us
    all_gather x1, waiting for transfers between devices, local(): gathered = lax.all_gather(normed, DP, axis=1, tiled=True)  94.9 us
    psum x1, blocking collectives, local(): total = lax.psum(local_total, DP_EXPERT)  64.8 us
    dot_general x1, matrix products, local(): jnp.einsum('ekt,etf->kef', reduced, cotangent, preferred_element_type=jnp...  9.85 us
  transfers between devices with their start and end apart: 4, of which 4 were waited for; matrix products, arithmetic and copies ran while one was open for 0% of the time, Pallas kernels for 0%

profile of v1, /device:TPU:0, one launch (start us, length us, event | category | flops | bytes accessed | tf_op | source)
XLA Modules:
  0.0 327.7 jit_solution(4464161766576310578)
XLA Ops:
  7.2 0.0 copy-start
  7.2 0.0 reduce-scatter.4.cloned.1.call-start
  7.2 1.5 copy-done
  8.8 3.5 %fusion.7 = bf16[256,512]{1,0:T(8,128)(2,1)S(1)} fusion(bf16[1,512,4096]{2,1,0:T(8,128)(2,1)} %param.6, bf16[1,4096,256]{2,1,0:T(8,128)(2,1)S(1)} %copy-done), kind=kOutput, calls=%fused_computation.9 | convolution fusion | flops 1073872896 | bytes 6553600 | tf_op jit(solution)/shard_map/etd,edr->ert/dot_general | solution.py:43
  12.2 9.8 %convolution_convert_fusion = bf16[256,14336]{1,0:T(8,128)(2,1)S(1)} fusion(bf16[256,512]{1,0:T(8,128)(2,1)S(1)} %fusion.7, bf16[1,512,14336]{2,1,0:T(8,128)(2,1)} %param.7), kind=kOutput, calls=%fused_computation | convolution fusion | flops 3761766400 | bytes 22282240 | tf_op jit(solution)/shard_map/ekt,etf->kef/dot_general | solution.py:47
  22.1 3.7 %copy.9 = bf16[4,4,2,8,1,14336]{5,3,2,1,0,4:T(8,128)(2,1)} copy(bf16[4,4,2,8,1,14336]{5,3,1,2,0,4:T(8,128)(2,1)S(1)} %bitcast.47) | data formatting | bytes 14680064 | tf_op jit(solution)/shard_map/transpose | solution.py:18
  25.8 0.0 copy-start.1
  25.8 0.0 copy-start.2
  25.8 0.0 reduce-scatter.4.cloned.1.call-update
  25.9 0.0 reduce-scatter.6.cloned.1.call-start
  25.9 75.4 %reduce-scatter.4.cloned.1.call-done = bf16[8,8,1,14336]{3,1,2,0:T(8,128)(2,1)} async-done(((bf16[32,8,1,14336]{3,1,2,0:T(8,128)(2,1)}), bf16[8,8,1,14336]{3,1,2,0:T(8,128)(2,1)}) %reduce-scatter.4.cloned.1.call-update) | async-done | bytes 1835024 | tf_op jit(solution)/shard_map/reduce_scatter | solution.py:20
  101.3 0.0 reduce-scatter.6.cloned.1.call-update
  101.3 0.0 reduce-scatter.8.cloned.1.call-start
  101.3 29.5 %reduce-scatter.6.cloned.1.call-done = bf16[2,8,1,14336]{3,1,2,0:T(8,128)(2,1)} async-done(((bf16[8,8,1,14336]{3,1,2,0:T(8,128)(2,1)}), bf16[2,8,1,14336]{3,1,2,0:T(8,128)(2,1)}) %reduce-scatter.6.cloned.1.call-update) | async-done | bytes 458768 | tf_op jit(solution)/shard_map/reduce_scatter | solution.py:20
  130.8 0.0 reduce-scatter.8.cloned.1.call-update
  130.8 0.0 all-gather.2.cloned.1.call-start
  131.6 19.3 %reduce-scatter.8.cloned.1.call-done = bf16[1,8,1,14336]{3,1,2,0:T(8,128)(2,1)} async-done(((bf16[2,8,1,14336]{3,1,2,0:T(8,128)(2,1)}), bf16[1,8,1,14336]{3,1,2,0:T(8,128)(2,1)}) %reduce-scatter.8.cloned.1.call-update) | async-done | bytes 229392 | tf_op jit(solution)/shard_map/reduce_scatter | solution.py:20
  150.9 1.7 fusion.12
  152.6 64.8 %psum.7 = f32[]{:T(128)} all-reduce(f32[]{:T(128)} %fusion.12), channel_id=1, replica_groups=mesh['dp_0'=4,'dp_1'=2,'dp_2'=4,'expert_0'=2,'expert_1'=2] {'dp_0','dp_1..., use_global_device_ids=true, to_apply=%region_4.0 | all-reduce | flops 1 | bytes 8 | tf_op jit(solution)/shard_map/psum | solution.py:56
  218.1 0.0 copy-done.1
  218.1 0.0 copy-done.2
  218.1 2.1 divide_convert_fusion
  220.2 0.0 all-gather.2.cloned.1.call-update
  220.3 94.9 %all-gather.2.cloned.1.call-done = bf16[1,256,14336]{2,1,0:T(8,128)(2,1)} async-done(((bf16[1,8,14336]{2,1,0:T(8,128)(2,1)}), bf16[1,256,14336]{2,1,0:T(8,128)(2,1)}) %all-gather.2.cloned.1.call-update) | async-done | bytes 7340048 | tf_op jit(solution)/shard_map/all_gather | solution.py:69
  315.1 6.1 %fusion.1 = bf16[1,128,14336]{2,1,0:T(8,128)(2,1)} fusion(bf16[1,256,14336]{2,1,0:T(8,128)(2,1)} %all-gather.2.cloned.1.call-done, bf16[1,4096,256]{2,1,0:T(8,128)(2,1)S(1)} %copy-done, s32[]{:T(128)S(6)} %select_n.3), kind=kOutput, calls=%fused_computation.3 | convolution fusion | flops 943194112 | bytes 11075588 | tf_op jit(solution)/shard_map/edk,ekf->edf/dot_general | solution.py:70
Async XLA Ops:
  7.2 1.6 copy-start
  7.2 94.1 %reduce-scatter.4.cloned.1.call-start = ((), (), s32[]{:S(2)}) async-start(), calls=%async_computation.3 | async-start | bytes 9175040 | tf_op jit(solution)/shard_map/reduce_scatter | solution.py:20
  25.8 192.3 %copy-start.1 = (f32[1,8,14336]{2,1,0:T(8,128)S(1)}, f32[1,8,14336]{2,1,0:T(8,128)}, u32[]{:S(2)}) copy-start(f32[1,8,14336]{2,1,0:T(8,128)} %param.10) | copy-start | bytes 1376260
  25.8 192.3 %copy-start.2 = (f32[1,8,14336]{2,1,0:T(8,128)S(1)}, f32[1,8,14336]{2,1,0:T(8,128)}, u32[]{:S(2)}) copy-start(f32[1,8,14336]{2,1,0:T(8,128)} %param.9) | copy-start | bytes 1376260
  25.9 105.0 %reduce-scatter.6.cloned.1.call-start = ((), (), s32[]{:S(2)}) async-start(), calls=%async_computation.4 | async-start | bytes 2293760 | tf_op jit(solution)/shard_map/reduce_scatter | solution.py:20
  101.3 49.6 %reduce-scatter.8.cloned.1.call-start = ((), (), s32[]{:S(2)}) async-start(), calls=%async_computation.5 | async-start | bytes 688128 | tf_op jit(solution)/shard_map/reduce_scatter | solution.py:20
  130.8 184.3 %all-gather.2.cloned.1.call-start = ((), (), s32[]{:S(2)}) async-start(), calls=%async_computation.6 | async-start | bytes 7569408 | tf_op jit(solution)/shard_map/all_gather | solution.py:69
Sparse Core Ops, SparseCore 0:
  26.0 75.2 reduce-scatter.3
  103.7 27.0 reduce-scatter.5
  133.2 17.6 reduce-scatter.7
  220.4 94.7 all-gather.1

commit v2 on v0

v2 whole, which is shorter than its diff:
```python
import functools

import jax
import jax.numpy as jnp
from jax import lax
from jax.experimental import pallas as pl
from jax.experimental.pallas import tpu as pltpu
from jax.sharding import Mesh
from jax.sharding import PartitionSpec as P

AXES = ("dp_0", "dp_1", "dp_2", "expert_0", "expert_1")
DP = ("dp_0", "dp_1", "dp_2")
EXPERT = ("expert_0", "expert_1")
MESH_ID = pl.DeviceIdType.MESH
RING = 4
FLOWS = 4
F32 = jnp.float32
BF16 = jnp.bfloat16


def powers(base, steps):
    value = jnp.ones(steps.shape, F32)
    for bit in range(8):
        on = (steps // (2**bit)) % 2
        value = value * jnp.where(on == 1, jnp.full(steps.shape, base ** (2**bit), F32), 1.0)
    return value


def step_kernel(
    groups, strip, limit,
    step_ref, reduced_ref, cot_hbm, basis_hbm, first_hbm, second_hbm,
    update_hbm, new_first_hbm, new_second_hbm,
    cot, own, ra, rb, rc, mix, own2, ra2, rb2, rc2, mix2, ysend, yrecv, sums,
    first, second, rows, perm, gath, nsend, nrecv, out, acc, near, acc2, far,
    rs_recv, rsy_recv, ag_recv, agy_recv, send, ysem, cot_sem, in_sem, near_sem, near_send,
    far_sem, far_send, out_sem,
):
    z, h, x = lax.axis_index("dp_0"), lax.axis_index("dp_1"), lax.axis_index("dp_2")
    lo, core = lax.axis_index("expert_0"), lax.axis_index("expert_1")
    width = FLOWS * strip
    ff = groups * width
    nrow = rows.shape[0]

    def turn(p, k):
        return lax.rem(p + (k % RING), RING)

    def at(zz, xx):
        return (zz, h, xx, lo, core)

    def major(f):
        return z if f % 2 == 0 else x

    def minor(f):
        return x if f % 2 == 0 else z

    def along_major(f, k):
        return at(turn(z, k), x) if f % 2 == 0 else at(z, turn(x, k))

    def along_minor(f, k):
        return at(z, turn(x, k)) if f % 2 == 0 else at(turn(z, k), x)

    def sense(f):
        return 1 if f < 2 else -1

    def remote(src, dst, ssem, rsem, dev):
        return pltpu.make_async_remote_copy(
            src_ref=src, dst_ref=dst, send_sem=ssem, recv_sem=rsem, device_id=dev, device_id_type=MESH_ID
        )

    def arrived(ref, sem):
        pltpu.make_async_copy(ref, ref, sem).wait()

    plane = [at(turn(z, k // RING), turn(x, k % RING)) for k in range(1, RING * RING)]
    column = [
        (z, lax.rem(h + (k // 4), 2), x, lax.rem(lo + (k // 2) % 2, 2), lax.rem(core + k % 2, 2))
        for k in range(1, 8)
    ]
    partner = (z, 1 - h, x, lo, core)

    barrier = pltpu.get_barrier_semaphore()
    for dev in plane + column:
        pl.semaphore_signal(barrier, inc=1, device_id=dev, device_id_type=MESH_ID)

    def cot_copy(t):
        cols = pl.ds(pl.multiple_of(t * width, width), width)
        return pltpu.make_async_copy(cot_hbm.at[0, :, cols], cot.at[t % 3], cot_sem.at[t % 3])

    for t in range(min(2, groups)):
        cot_copy(t).start()
    dp_index = z * (2 * RING) + h * RING + x
    loads = [
        pltpu.make_async_copy(first_hbm.at[0], first, in_sem.at[0]),
        pltpu.make_async_copy(second_hbm.at[0], second, in_sem.at[1]),
        pltpu.make_async_copy(
            basis_hbm.at[0, pl.ds(pl.multiple_of(dp_index * nrow, nrow), nrow), :], rows, in_sem.at[2]
        ),
    ]
    for load in loads:
        load.start()
    acc[...] = jnp.zeros_like(acc)
    pl.semaphore_wait(barrier, len(plane) + len(column))

    @pl.loop(0, groups + 5)
    def _(t):
        @pl.when(t < groups)
        def _():
            @pl.when(t + 2 < groups)
            def _():
                cot_copy(t + 2).start()

            cot_copy(t).wait()
            for f in range(FLOWS):
                part = jnp.dot(
                    reduced_ref[...], cot[t % 3, :, f * strip : (f + 1) * strip], preferred_element_type=F32
                )
                for u in range(RING):
                    for v in range(RING):
                        zz, xx = (u, v) if f % 2 == 0 else (v, u)
                        r0 = zz * 64 + xx * 8
                        own[f, t, u, v * 16 : (v + 1) * 16, :] = jnp.concatenate(
                            [part[r0 : r0 + 8], part[r0 + 32 : r0 + 40]], axis=0
                        ).astype(BF16)
                d = sense(f)
                p = major(f)
                remote(
                    own.at[f, t, turn(p, 2)], rb.at[f, t], send.at[1], rs_recv.at[1, f, t], along_major(f, -d)
                ).start()
                remote(
                    own.at[f, t, turn(p, d)], ra.at[f, t], send.at[0], rs_recv.at[0, f, t], along_major(f, d)
                ).start()

        @pl.when(jnp.logical_and(t >= 1, t < groups + 1))
        def _():
            s = t - 1
            for f in range(FLOWS):
                d = sense(f)
                arrived(rb.at[f, s], rs_recv.at[1, f, s])
                mix[f, s] = (own[f, s, turn(major(f), -d)].astype(F32) + rb[f, s].astype(F32)).astype(BF16)
                remote(
                    mix.at[f, s], rc.at[f, s], send.at[2], rs_recv.at[2, f, s], along_major(f, -d)
                ).start()

        @pl.when(jnp.logical_and(t >= 2, t < groups + 2))
        def _():
            s = t - 2
            for f in range(FLOWS):
                d = sense(f)
                q = minor(f)
                arrived(ra.at[f, s], rs_recv.at[0, f, s])
                arrived(rc.at[f, s], rs_recv.at[2, f, s])
                whole = own[f, s, major(f)].astype(F32) + ra[f, s].astype(F32) + rc[f, s].astype(F32)
                for v in range(RING):
                    own2[f, s, v] = whole[v * 16 : (v + 1) * 16].astype(BF16)
                remote(
                    own2.at[f, s, turn(q, 2)], rb2.at[f, s], send.at[4], rs_recv.at[4, f, s], along_minor(f, -d)
                ).start()
                remote(
                    own2.at[f, s, turn(q, d)], ra2.at[f, s], send.at[3], rs_recv.at[3, f, s], along_minor(f, d)
                ).start()

        @pl.when(jnp.logical_and(t >= 3, t < groups + 3))
        def _():
            s = t - 3
            for f in range(FLOWS):
                d = sense(f)
                arrived(rb2.at[f, s], rs_recv.at[4, f, s])
                mix2[f, s] = (own2[f, s, turn(minor(f), -d)].astype(F32) + rb2[f, s].astype(F32)).astype(BF16)
                remote(
                    mix2.at[f, s], rc2.at[f, s], send.at[5], rs_recv.at[5, f, s], along_minor(f, -d)
                ).start()

        @pl.when(jnp.logical_and(t >= 4, t < groups + 4))
        def _():
            s = t - 4
            for f in range(FLOWS):
                arrived(ra2.at[f, s], rs_recv.at[3, f, s])
                arrived(rc2.at[f, s], rs_recv.at[5, f, s])
                whole = own2[f, s, minor(f)].astype(F32) + ra2[f, s].astype(F32) + rc2[f, s].astype(F32)
                low = h == 0
                sums[s, f * 8 : (f + 1) * 8, :] = jnp.where(low, whole[:8], whole[8:])
                other = jnp.where(low, whole[8:], whole[:8])
                if f % 2 == 0:
                    held = other
                else:
                    ysend[s, (f - 1) * 8 : (f + 1) * 8, :] = jnp.concatenate([held, other], axis=0).astype(BF16)
            remote(ysend.at[s], yrecv.at[s], ysem.at[0], rsy_recv.at[s], partner).start()

        @pl.when(t >= 5)
        def _():
            s = t - 5
            arrived(yrecv.at[s], rsy_recv.at[s])
            grad = sums[s] + yrecv[s].astype(F32)
            sums[s] = grad
            square = grad * grad
            piece = acc[...]
            for i in range(FLOWS):
                for j in range(strip // 128):
                    piece = piece + square[i * 8 : (i + 1) * 8, j * 128 : (j + 1) * 128]
            acc[...] = piece

    for k, dev in enumerate(plane):
        remote(acc, near.at[k], near_send.at[k], near_sem.at[k], dev).start()
    for load in loads:
        load.wait()
    for o in range(2):
        r = lax.broadcasted_iota(jnp.int32, (256, 256), 0)
        q = lax.broadcasted_iota(jnp.int32, (256, 256), 1)
        u, v = q // 64, (q // 16) % 4
        zz, xx = (u, v) if o == 0 else (v, u)
        place = zz * 64 + ((q // 8) % 2) * 32 + xx * 8 + q % 8
        one = jnp.where(place == r, 1.0, 0.0).astype(BF16)
        perm[o] = jnp.dot(rows[...], one, preferred_element_type=F32).astype(BF16)
    steps = jnp.full((8, 128), step_ref[0], jnp.int32)
    corr_one = 1.0 - powers(0.9, steps)
    corr_two = 1.0 - powers(0.999, steps)
    total = acc[...]
    for k in range(len(plane)):
        arrived(near.at[k], near_sem.at[k])
        total = total + near[k]
    acc2[...] = total
    for k, dev in enumerate(column):
        remote(acc2, far.at[k], far_send.at[k], far_sem.at[k], dev).start()
    for k in range(len(column)):
        arrived(far.at[k], far_sem.at[k])
        total = total + far[k]
    total = jnp.sum(jnp.sum(total, axis=1, keepdims=True), axis=0, keepdims=True)
    factor = jnp.minimum(1.0, limit / jnp.sqrt(total + 1e-06))
    inv_one = jnp.max(1.0 / corr_one, axis=(0, 1), keepdims=True)
    inv_two = jnp.max(1.0 / corr_two, axis=(0, 1), keepdims=True)

    @pl.loop(0, groups + 5)
    def _(t):
        @pl.when(t < groups)
        def _():
            for f in range(FLOWS):
                cols = pl.ds(pl.multiple_of(t * width + f * strip, strip), strip)
                grad = sums[t, f * 8 : (f + 1) * 8, :] * factor
                one = 0.9 * first[:, cols] + 0.1 * grad
                two = 0.999 * second[:, cols] + 0.001 * grad * grad
                first[:, cols] = one
                second[:, cols] = two
                normed = (one * inv_one) / (jnp.sqrt(two * inv_two) + 1e-08)
                if f % 2 == 0:
                    held = normed
                else:
                    nsend[t, (f - 1) * 8 : (f + 1) * 8, :] = jnp.concatenate([held, normed], axis=0).astype(BF16)
            remote(nsend.at[t], nrecv.at[t], ysem.at[1], agy_recv.at[t], partner).start()

        @pl.when(jnp.logical_and(t >= 1, t < groups + 1))
        def _():
            s = t - 1
            arrived(nrecv.at[s], agy_recv.at[s])
            low = h == 0
            mine, theirs = nsend[s].astype(F32), nrecv[s].astype(F32)
            top, bottom = jnp.where(low, mine, theirs), jnp.where(low, theirs, mine)
            for f in range(FLOWS):
                d = sense(f)
                u, v = major(f), minor(f)
                gath[f, s, u, v] = jnp.concatenate(
                    [top[f * 8 : (f + 1) * 8], bottom[f * 8 : (f + 1) * 8]], axis=0
                ).astype(BF16)
                block = gath.at[f, s, u, v]
                remote(block, block, send.at[7], ag_recv.at[1, f, s], along_minor(f, -d)).start()
                remote(block, block, send.at[6], ag_recv.at[0, f, s], along_minor(f, d)).start()

        @pl.when(jnp.logical_and(t >= 2, t < groups + 2))
        def _():
            s = t - 2
            for f in range(FLOWS):
                d = sense(f)
                block = gath.at[f, s, major(f), turn(minor(f), d)]
                arrived(block, ag_recv.at[1, f, s])
                remote(block, block, send.at[8], ag_recv.at[2, f, s], along_minor(f, -d)).start()

        @pl.when(jnp.logical_and(t >= 3, t < groups + 3))
        def _():
            s = t - 3
            for f in range(FLOWS):
                d = sense(f)
                u, v = major(f), minor(f)
                arrived(gath.at[f, s, u, turn(v, -d)], ag_recv.at[0, f, s])
                arrived(gath.at[f, s, u, turn(v, 2)], ag_recv.at[2, f, s])
                block = gath.at[f, s, u]
                remote(block, block, send.at[10], ag_recv.at[4, f, s], along_major(f, -d)).start()
                remote(block, block, send.at[9], ag_recv.at[3, f, s], along_major(f, d)).start()

        @pl.when(jnp.logical_and(t >= 4, t < groups + 4))
        def _():
            s = t - 4
            for f in range(FLOWS):
                d = sense(f)
                block = gath.at[f, s, turn(major(f), d)]
                arrived(block, ag_recv.at[4, f, s])
                remote(block, block, send.at[11], ag_recv.at[5, f, s], along_major(f, -d)).start()

        @pl.when(t >= 5)
        def _():
            s = t - 5
            for f in range(FLOWS):
                d = sense(f)
                u = major(f)
                arrived(gath.at[f, s, turn(u, -d)], ag_recv.at[3, f, s])
                arrived(gath.at[f, s, turn(u, 2)], ag_recv.at[5, f, s])
                product = jnp.dot(perm[f % 2], gath[f, s].reshape(256, strip), preferred_element_type=F32)
                out[s, :, f * strip : (f + 1) * strip] = (0.25 * product).astype(BF16)
            cols = pl.ds(pl.multiple_of(s * width, width), width)
            pltpu.make_async_copy(out.at[s], update_hbm.at[0, :, cols], out_sem.at[2, s]).start()

    stores = [
        pltpu.make_async_copy(first, new_first_hbm.at[0], out_sem.at[0, 0]),
        pltpu.make_async_copy(second, new_second_hbm.at[0], out_sem.at[1, 0]),
    ]
    for store in stores:
        store.start()
    for k in range(len(plane)):
        arrived(acc, near_send.at[k])
    for k in range(len(column)):
        arrived(acc2, far_send.at[k])
    for k in (0, 1, 2, 9, 10, 11):
        arrived(ra, send.at[k])
    for k in (3, 4, 5, 6, 7, 8):
        arrived(ra2, send.at[k])
    for k in range(2):
        arrived(yrecv, ysem.at[k])
    for s in range(groups):
        pltpu.make_async_copy(out.at[s], update_hbm.at[0, :, s * width : (s + 1) * width], out_sem.at[2, s]).wait()
    for store in stores:
        store.wait()


def fused(step_count, reduced, cotangent, basis, first, second, groups, total_entries):
    _, tokens, ff = cotangent.shape
    strip = ff // groups // FLOWS
    width = FLOWS * strip
    n_dp = 2 * RING * RING
    out_rows = basis.shape[1] // n_dp
    any_space = pl.BlockSpec(memory_space=pl.ANY)
    limit = 0.25 * total_entries**0.5
    dma = pltpu.SemaphoreType.DMA
    big = pltpu.VMEM((FLOWS, groups, 64, strip), BF16)
    small = pltpu.VMEM((FLOWS, groups, 16, strip), BF16)
    yshape = (groups, 32, strip)
    return pl.pallas_call(
        functools.partial(step_kernel, groups, strip, limit),
        out_shape=(
            jax.ShapeDtypeStruct((1, out_rows, ff), BF16),
            jax.ShapeDtypeStruct(first.shape, F32),
            jax.ShapeDtypeStruct(second.shape, F32),
        ),
        in_specs=[
            pl.BlockSpec(memory_space=pltpu.SMEM),
            pl.BlockSpec(memory_space=pltpu.VMEM),
            any_space, any_space, any_space, any_space,
        ],
        out_specs=(any_space, any_space, any_space),
        scratch_shapes=[
            pltpu.VMEM((3, tokens, width), BF16),
            pltpu.VMEM((FLOWS, groups, RING, 64, strip), BF16),
            big, big, big, big,
            pltpu.VMEM((FLOWS, groups, RING, 16, strip), BF16),
            small, small, small, small,
            pltpu.VMEM(yshape, BF16),
            pltpu.VMEM(yshape, BF16),
            pltpu.VMEM(yshape, F32),
            pltpu.VMEM((8, ff), F32),
            pltpu.VMEM((8, ff), F32),
            pltpu.VMEM((out_rows, 256), BF16),
            pltpu.VMEM((2, out_rows, 256), BF16),
            pltpu.VMEM((FLOWS, groups, RING, RING, 16, strip), BF16),
            pltpu.VMEM(yshape, BF16),
            pltpu.VMEM(yshape, BF16),
            pltpu.VMEM((groups, out_rows, width), BF16),
            pltpu.VMEM((8, 128), F32),
            pltpu.VMEM((15, 8, 128), F32),
            pltpu.VMEM((8, 128), F32),
            pltpu.VMEM((7, 8, 128), F32),
            dma((6, FLOWS, groups)),
            dma((groups,)),
            dma((6, FLOWS, groups)),
            dma((groups,)),
            dma((12,)),
            dma((2,)),
            dma((3,)),
            dma((3,)),
            dma((15,)),
            dma((15,)),
            dma((7,)),
            dma((7,)),
            dma((3, groups)),
        ],
        compiler_params=pltpu.CompilerParams(
            collective_id=0, has_side_effects=True, vmem_limit_bytes=63 * 1024 * 1024
        ),
        name="galore_step",
    )(step_count, reduced, cotangent, basis, first, second)


def make_local(groups, total_entries):
    def local(acts, cotangent, basis, first_moment, second_moment, step_count):
        reduced = jnp.einsum("td,dr->rt", acts[0], basis[0], preferred_element_type=F32).astype(BF16)
        return fused(step_count, reduced, cotangent, basis, first_moment, second_moment, groups, total_entries)

    return local


def solution(mesh, groups=7, total_entries=4 * 256 * 14336):
    split = Mesh(mesh.devices.reshape(4, 2, 4, 2, 2), AXES)
    return jax.shard_map(
        make_local(groups, total_entries),
        mesh=split,
        in_specs=(
            P(EXPERT, DP, None),
            P(EXPERT, DP, None),
            P(EXPERT, None, None),
            P(EXPERT, DP, None),
            P(EXPERT, DP, None),
            P(),
        ),
        out_specs=(P(EXPERT, DP, None), P(EXPERT, DP, None), P(EXPERT, DP, None)),
        check_vma=False,
    )
```

time: 390 us -> 130 us (0.33)
  waiting for transfers between devices: 296 us -> 0 us
  Pallas kernels: 0 us -> 118 us
  blocking collectives: 38 us -> 0 us
  matrix products: 22.3 us -> 4.83 us
  between operations: 15.2 us -> 1.3 us
  local copies, waits for them, and re-layouts: 13.5 us -> 5.82 us
  other arithmetic: 3.91 us -> 0 us
    reduce_scatter x3 -> x0, waiting for transfers between devices: 203 us -> none  [reduced_to_own(): blocks = lax.psum_scatter(blocks, axes[k], scatter_dimension=0, tiled=True)]
    pallas_call x0 -> x1, Pallas kernels: none -> 118 us  [fused(): pl.pallas_call(functools.partial(step_kernel, groups, strip, limit), out_...]
    all_gather x1 -> x0, waiting for transfers between devices: 92.6 us -> none  [local(): gathered = lax.all_gather(normed, DP, axis=1, tiled=True)]
    psum x5 -> x0, blocking collectives: 38 us -> none  [one_axis_at_a_time(): array = lax.psum(array, axis)]
    dot_general x3 -> x1, matrix products: 22.3 us -> 4.83 us  [local(): jnp.einsum('td,dr->rt', acts[0], basis[0], preferred_element_type=F32)]
    transpose x1 -> x0, local copies, waits for them, and re-layouts: 12 us -> none  [reduced_to_own(): jnp.moveaxis(blocks, sequence, range(len(axes))).reshape(-1, *inside)]
    unnamed x6 -> x7, local copies, waits for them, and re-layouts: 1.55 us -> 5.82 us
  transfers between devices with their start and end apart: 4 -> 0, of which waited for: 4 -> 0; matrix products, arithmetic and copies ran while one was open for 0% -> 0% of each run, Pallas kernels for 0% -> 0%
where the time goes in v2:
time: 130 us
  Pallas kernels  118 us (91%)
  local copies, waits for them, and re-layouts  5.82 us (4%)
  matrix products  4.83 us (4%)
  between operations  1.3 us (1%)
    pallas_call x1, Pallas kernels, fused(): pl.pallas_call(functools.partial(step_kernel, groups, strip, limit), out_...  118 us
    unnamed x7, local copies, waits for them, and re-layouts  5.82 us
    dot_general x1, matrix products, local(): jnp.einsum('td,dr->rt', acts[0], basis[0], preferred_element_type=F32)  4.83 us

profile of v2, /device:TPU:0, one launch (start us, length us, event | category | flops | bytes accessed | tf_op | source)
XLA Modules:
  0.0 129.6 jit_solution(1205662830838098412)
XLA Ops:
  1.3 4.8 %fusion.3.reduced_ref = bf16[256,512]{1,0:T(8,128)(2,1)} fusion(bf16[1,512,4096]{2,1,0:T(8,128)(2,1)} %param.6, bf16[1,4096,256]{2,1,0:T(8,128)(2,1)} %basis_hbm.1), kind=kOutput, calls=%fused_computation.3 | convolution fusion | flops 1073872896 | bytes 6553600 | tf_op jit(solution)/shard_map/td,dr->rt/dot_general | solution.py:400
  6.1 117.6 %galore_step.1 = (bf16[1,128,14336]{2,1,0:T(8,128)(2,1)}, f32[1,8,14336]{2,1,0:T(8,128)}, f32[1,8,14336]{2,1,0:T(8,128)}) custom-call(s32[1]{0:T(128)S(6)} %copy.12.step_ref, bf16[256,512]{1,0:T(8,128)(2,1)} %fusion.3.reduced_ref, bf16[1,512,14336]{2,1,0:T(8,128)(2,1)} %cot_hbm.1, bf16[1,4096,256]{2,1,0:T(8,128)(2,1)} %basis_hbm.1, ...), custom_call_target="tpu_custom_call" | custom-call | tf_op jit(solution)/shard_map/galore_step/pallas_call | solution.py:343
  123.7 0.0 copy-start.1
  123.7 0.0 copy-start
  123.7 4.3 %copy.13 = bf16[1,128,14336]{2,1,0:T(8,128)(2,1)} copy(bf16[1,128,14336]{2,1,0:T(8,128)(2,1)} %get-tuple-element.6) | data formatting | bytes 7340032
  128.0 0.0 copy-done.1
  128.0 0.8 copy.14
  128.8 0.0 copy-done
  128.8 0.8 copy.15
Async XLA Ops:
  123.7 4.3 %copy-start.1 = (f32[1,8,14336]{2,1,0:T(8,128)S(1)}, f32[1,8,14336]{2,1,0:T(8,128)}, u32[]{:S(2)}) copy-start(f32[1,8,14336]{2,1,0:T(8,128)} %get-tuple-element.7) | copy-start | bytes 1376260
  123.7 5.1 %copy-start = (f32[1,8,14336]{2,1,0:T(8,128)S(1)}, f32[1,8,14336]{2,1,0:T(8,128)}, u32[]{:S(2)}) copy-start(f32[1,8,14336]{2,1,0:T(8,128)} %get-tuple-element.8) | copy-start | bytes 1376260

commit v3 on v2

v3 whole, which is shorter than its diff:
```python
import functools

import jax
import jax.numpy as jnp
from jax import lax
from jax.experimental import pallas as pl
from jax.experimental.pallas import tpu as pltpu
from jax.sharding import Mesh
from jax.sharding import PartitionSpec as P

AXES = ("dp_0", "dp_1", "dp_2", "expert_0", "expert_1")
DP = ("dp_0", "dp_1", "dp_2")
EXPERT = ("expert_0", "expert_1")
MESH_ID = pl.DeviceIdType.MESH
RING = 4
FLOWS = 4
F32 = jnp.float32
BF16 = jnp.bfloat16


def powers(base, steps):
    value = jnp.ones(steps.shape, F32)
    for bit in range(8):
        on = (steps // (2**bit)) % 2
        value = value * jnp.where(on == 1, jnp.full(steps.shape, base ** (2**bit), F32), 1.0)
    return value


def step_kernel(
    plain, strip, limit,
    step_ref, acts_hbm, cot_hbm, basis_hbm, first_hbm, second_hbm,
    update_hbm, new_first_hbm, new_second_hbm,
    acts, basis, total_acc, reduced, cot, ycot,
    own, ra, rb, rc, mix, own2, ra2, rb2, rc2, mix2, ysend, yrecv, sums,
    yown, ypass, ypart, ysums, first, second, perm, yperm, gath, nsend, nrecv, gpass, gpart, out, yout,
    acc, near, acc2, far,
    rs_recv, rsy_recv, ag_recv, agy_recv, send, ysem, pass_recv, part_recv, gpass_recv, gpart_recv, pass_send,
    cot_sem, ycot_sem, in_sem, near_sem, near_send, far_sem, far_send, out_sem,
):
    z, h, x = lax.axis_index("dp_0"), lax.axis_index("dp_1"), lax.axis_index("dp_2")
    lo, core = lax.axis_index("expert_0"), lax.axis_index("expert_1")
    width = FLOWS * strip
    pair = 2 * strip
    base = plain * width
    steps_all = plain + 1
    nrow = out.shape[1]
    dp_index = z * (2 * RING) + h * RING + x

    def turn(p, k):
        return lax.rem(p + (k % RING), RING)

    def at(zz, xx):
        return (zz, h, xx, lo, core)

    def major(f):
        return z if f % 2 == 0 else x

    def minor(f):
        return x if f % 2 == 0 else z

    def along_major(f, k):
        return at(turn(z, k), x) if f % 2 == 0 else at(z, turn(x, k))

    def along_minor(f, k):
        return at(z, turn(x, k)) if f % 2 == 0 else at(turn(z, k), x)

    def sense(f):
        return 1 if f < 2 else -1

    up = (z, lax.rem(h + lo, 2), x, 1 - lo, core)
    down = (z, lax.rem(h + 1 + lo, 2), x, 1 - lo, core)

    def along_y(f):
        return up if f < 2 else down

    def remote(src, dst, ssem, rsem, dev):
        return pltpu.make_async_remote_copy(
            src_ref=src, dst_ref=dst, send_sem=ssem, recv_sem=rsem, device_id=dev, device_id_type=MESH_ID
        )

    def arrived(ref, sem):
        pltpu.make_async_copy(ref, ref, sem).wait()

    plane = [at(turn(z, k // RING), turn(x, k % RING)) for k in range(1, RING * RING)]
    column = [
        (z, lax.rem(h + (k // 4), 2), x, lax.rem(lo + (k // 2) % 2, 2), lax.rem(core + k % 2, 2))
        for k in range(1, 8)
    ]
    partner = (z, 1 - h, x, lo, core)

    barrier = pltpu.get_barrier_semaphore()
    for dev in plane + column:
        pl.semaphore_signal(barrier, inc=1, device_id=dev, device_id_type=MESH_ID)

    def cot_copy(t):
        cols = pl.ds(pl.multiple_of(t * width, width), width)
        return pltpu.make_async_copy(cot_hbm.at[0, :, cols], cot.at[t % 3], cot_sem.at[t % 3])

    deep = acts.shape[0]
    kdim = acts.shape[2]
    first_loads = []
    for k in range(deep):
        span = pl.ds(k * kdim, kdim)
        first_loads.append(
            (
                pltpu.make_async_copy(acts_hbm.at[0, :, span], acts.at[k], in_sem.at[2 + 2 * k]),
                pltpu.make_async_copy(basis_hbm.at[0, span, :], basis.at[span, :], in_sem.at[3 + 2 * k]),
            )
        )
    for one, two in first_loads:
        two.start()
        one.start()
    cot_copy(0).start()
    ycot_copy = pltpu.make_async_copy(cot_hbm.at[0, :, base : base + FLOWS * pair], ycot, ycot_sem)
    ycot_copy.start()
    cot_copy(1).start()
    loads = [
        pltpu.make_async_copy(first_hbm.at[0], first, in_sem.at[0]),
        pltpu.make_async_copy(second_hbm.at[0], second, in_sem.at[1]),
    ]
    for load in loads:
        load.start()
    acc[...] = jnp.zeros_like(acc)
    for k, (one, two) in enumerate(first_loads):
        two.wait()
        one.wait()
        piece = jnp.dot(acts[k], basis[k * kdim : (k + 1) * kdim, :], preferred_element_type=F32)
        if k == 0:
            total_acc[...] = piece
        else:
            total_acc[...] += piece
    reduced[...] = total_acc[...].T.astype(BF16)
    pl.semaphore_wait(barrier, len(plane) + len(column))

    def send_major(f, t):
        d = sense(f)
        p = major(f)
        remote(own.at[f, t, turn(p, 2)], rb.at[f, t], send.at[1], rs_recv.at[1, f, t], along_major(f, -d)).start()
        remote(own.at[f, t, turn(p, d)], ra.at[f, t], send.at[0], rs_recv.at[0, f, t], along_major(f, d)).start()

    @pl.loop(0, plain + 5)
    def _(t):
        @pl.when(t < plain)
        def _():
            @pl.when(jnp.logical_and(t >= 1, t + 1 < plain))
            def _():
                cot_copy(t + 1).start()

            cot_copy(t).wait()
            for f in range(FLOWS):
                part = jnp.dot(
                    reduced[...], cot[t % 3, :, f * strip : (f + 1) * strip], preferred_element_type=F32
                )
                for u in range(RING):
                    for v in range(RING):
                        zz, xx = (u, v) if f % 2 == 0 else (v, u)
                        r0 = zz * 64 + xx * 8
                        own[f, t, u, v * 16 : (v + 1) * 16, :] = jnp.concatenate(
                            [part[r0 : r0 + 8], part[r0 + 32 : r0 + 40]], axis=0
                        ).astype(BF16)
                send_major(f, t)

        @pl.when(t == 0)
        def _():
            ycot_copy.wait()
            for f in (0, 2, 1, 3):
                part = jnp.dot(reduced[...], ycot[:, f * pair : (f + 1) * pair], preferred_element_type=F32)
                for u in range(RING):
                    for v in range(RING):
                        zz, xx = (u, v) if f % 2 == 0 else (v, u)
                        for y in range(2):
                            r0 = zz * 64 + y * 32 + xx * 8
                            yown[f, y, u, v * 16 : (v + 1) * 16, :] = jnp.concatenate(
                                [part[r0 : r0 + 8, :strip], part[r0 : r0 + 8, strip:]], axis=0
                            ).astype(BF16)
                remote(yown.at[f, 1 - h], ypass.at[f], pass_send.at[0], pass_recv.at[f], along_y(f)).start()

        @pl.when(t == plain)
        def _():
            for f in range(FLOWS):
                arrived(ypart.at[f], part_recv.at[f])
                for u in range(RING):
                    own[f, plain, u] = (yown[f, h, u].astype(F32) + ypart[f, u].astype(F32)).astype(BF16)
                send_major(f, plain)

        @pl.when(jnp.logical_and(t >= 1, t < steps_all + 1))
        def _():
            s = t - 1
            for f in range(FLOWS):
                d = sense(f)
                arrived(rb.at[f, s], rs_recv.at[1, f, s])
                mix[f, s] = (own[f, s, turn(major(f), -d)].astype(F32) + rb[f, s].astype(F32)).astype(BF16)
                remote(
                    mix.at[f, s], rc.at[f, s], send.at[2], rs_recv.at[2, f, s], along_major(f, -d)
                ).start()

        @pl.when(jnp.logical_and(t >= 2, t < steps_all + 2))
        def _():
            s = t - 2
            for f in range(FLOWS):
                d = sense(f)
                q = minor(f)
                arrived(ra.at[f, s], rs_recv.at[0, f, s])
                arrived(rc.at[f, s], rs_recv.at[2, f, s])
                whole = own[f, s, major(f)].astype(F32) + ra[f, s].astype(F32) + rc[f, s].astype(F32)
                for v in range(RING):
                    own2[f, s, v] = whole[v * 16 : (v + 1) * 16].astype(BF16)
                remote(
                    own2.at[f, s, turn(q, 2)], rb2.at[f, s], send.at[4], rs_recv.at[4, f, s], along_minor(f, -d)
                ).start()
                remote(
                    own2.at[f, s, turn(q, d)], ra2.at[f, s], send.at[3], rs_recv.at[3, f, s], along_minor(f, d)
                ).start()

        for turn_of, flows in ((1, (0, 2)), (2, (1, 3))):

            @pl.when(t == turn_of)
            def _():
                for f in flows:
                    arrived(ypass.at[f], pass_recv.at[f])
                    remote(ypass.at[f], ypart.at[f], pass_send.at[1], part_recv.at[f], along_y(f)).start()

        @pl.when(jnp.logical_and(t >= 3, t < steps_all + 3))
        def _():
            s = t - 3
            for f in range(FLOWS):
                d = sense(f)
                arrived(rb2.at[f, s], rs_recv.at[4, f, s])
                mix2[f, s] = (own2[f, s, turn(minor(f), -d)].astype(F32) + rb2[f, s].astype(F32)).astype(BF16)
                remote(
                    mix2.at[f, s], rc2.at[f, s], send.at[5], rs_recv.at[5, f, s], along_minor(f, -d)
                ).start()

        def last_two(f, s):
            arrived(ra2.at[f, s], rs_recv.at[3, f, s])
            arrived(rc2.at[f, s], rs_recv.at[5, f, s])
            return own2[f, s, minor(f)].astype(F32) + ra2[f, s].astype(F32) + rc2[f, s].astype(F32)

        def add_squares(value):
            square = value * value
            piece = acc[...]
            for i in range(value.shape[0] // 8):
                for j in range(strip // 128):
                    piece = piece + square[i * 8 : (i + 1) * 8, j * 128 : (j + 1) * 128]
            acc[...] = piece

        @pl.when(jnp.logical_and(t >= 5, t < plain + 5))
        def _():
            s = t - 5
            arrived(yrecv.at[s], rsy_recv.at[s])
            grad = sums[s] + yrecv[s].astype(F32)
            sums[s] = grad
            add_squares(grad)

        @pl.when(jnp.logical_and(t >= 4, t < plain + 4))
        def _():
            s = t - 4
            for f in range(FLOWS):
                whole = last_two(f, s)
                low = h == 0
                sums[s, f * 8 : (f + 1) * 8, :] = jnp.where(low, whole[:8], whole[8:])
                other = jnp.where(low, whole[8:], whole[:8])
                if f % 2 == 0:
                    held = other
                else:
                    ysend[s, (f - 1) * 8 : (f + 1) * 8, :] = jnp.concatenate([held, other], axis=0).astype(BF16)
            remote(ysend.at[s], yrecv.at[s], ysem.at[0], rsy_recv.at[s], partner).start()

        @pl.when(t == plain + 4)
        def _():
            for f in range(FLOWS):
                whole = last_two(f, plain)
                ysums[f] = whole
                add_squares(whole)

    for k, dev in enumerate(plane):
        remote(acc, near.at[k], near_send.at[k], near_sem.at[k], dev).start()
    for load in loads:
        load.wait()
    rows = basis[pl.ds(pl.multiple_of(dp_index * nrow, nrow), nrow), :]
    r = lax.broadcasted_iota(jnp.int32, (256, 256), 0)
    q = lax.broadcasted_iota(jnp.int32, (256, 256), 1)
    for o in range(2):
        u, v = q // 64, (q // 16) % 4
        zz, xx = (u, v) if o == 0 else (v, u)
        place = zz * 64 + xx * 8 + q % 8
        half = (q // 8) % 2
        one = jnp.where(place + 32 * half == r, 1.0, 0.0).astype(BF16)
        perm[o] = jnp.dot(rows, one, preferred_element_type=F32).astype(BF16)
        for away in range(2):
            y = lax.rem(h + away, 2)
            for j in range(2):
                hit = jnp.logical_and(place + 32 * y == r, half == j)
                one = jnp.where(hit, 1.0, 0.0).astype(BF16)
                yperm[o, away, j] = jnp.dot(rows, one, preferred_element_type=F32).astype(BF16)
    steps = jnp.full((8, 128), step_ref[0], jnp.int32)
    corr_one = 1.0 - powers(0.9, steps)
    corr_two = 1.0 - powers(0.999, steps)
    total = acc[...]
    for k in range(len(plane)):
        arrived(near.at[k], near_sem.at[k])
        total = total + near[k]
    acc2[...] = total
    for k, dev in enumerate(column):
        remote(acc2, far.at[k], far_send.at[k], far_sem.at[k], dev).start()
    for k in range(len(column)):
        arrived(far.at[k], far_sem.at[k])
        total = total + far[k]
    total = jnp.sum(jnp.sum(total, axis=1, keepdims=True), axis=0, keepdims=True)
    factor = jnp.minimum(1.0, limit / jnp.sqrt(total + 1e-06))
    inv_one = jnp.max(1.0 / corr_one, axis=(0, 1), keepdims=True)
    inv_two = jnp.max(1.0 / corr_two, axis=(0, 1), keepdims=True)

    def adam(cols, sums_now):
        grad = sums_now * factor
        one = 0.9 * first[:, cols] + 0.1 * grad
        two = 0.999 * second[:, cols] + 0.001 * grad * grad
        first[:, cols] = one
        second[:, cols] = two
        return (one * inv_one) / (jnp.sqrt(two * inv_two) + 1e-08)

    def send_minor(f, a):
        d = sense(f)
        block = gath.at[f, a, major(f), minor(f)]
        remote(block, block, send.at[7], ag_recv.at[1, f, a], along_minor(f, -d)).start()
        remote(block, block, send.at[6], ag_recv.at[0, f, a], along_minor(f, d)).start()

    def y_place(f, k):
        return turn(major(f), (0, sense(f), -sense(f), 2)[k])

    def y_out(f, k):
        place = y_place(f, k)
        remote(
            gath.at[f, 0, place], gpass.at[f, place], pass_send.at[2], gpass_recv.at[f, k], along_y(f)
        ).start()

    def y_relay(f, k):
        place = y_place(f, k)
        arrived(gpass.at[f, place], gpass_recv.at[f, k])
        remote(
            gpass.at[f, place], gpart.at[f, place], pass_send.at[3], gpart_recv.at[f, k], along_y(f)
        ).start()

    for f in range(FLOWS):
        top = adam(pl.ds(base + f * pair, strip), ysums[f, :8])
        bottom = adam(pl.ds(base + f * pair + strip, strip), ysums[f, 8:])
        gath[f, 0, major(f), minor(f)] = jnp.concatenate([top, bottom], axis=0).astype(BF16)
        send_minor(f, 0)

    @pl.loop(0, plain + 5)
    def _(t):
        @pl.when(t < plain)
        def _():
            for f in range(FLOWS):
                cols = pl.ds(pl.multiple_of(t * width + f * strip, strip), strip)
                normed = adam(cols, sums[t, f * 8 : (f + 1) * 8, :])
                if f % 2 == 0:
                    held = normed
                else:
                    nsend[t, (f - 1) * 8 : (f + 1) * 8, :] = jnp.concatenate([held, normed], axis=0).astype(BF16)
            remote(nsend.at[t], nrecv.at[t], ysem.at[1], agy_recv.at[t], partner).start()

        @pl.when(jnp.logical_and(t >= 1, t < plain + 1))
        def _():
            s = t - 1
            arrived(nrecv.at[s], agy_recv.at[s])
            low = h == 0
            mine, theirs = nsend[s].astype(F32), nrecv[s].astype(F32)
            top, bottom = jnp.where(low, mine, theirs), jnp.where(low, theirs, mine)
            for f in range(FLOWS):
                gath[f, t, major(f), minor(f)] = jnp.concatenate(
                    [top[f * 8 : (f + 1) * 8], bottom[f * 8 : (f + 1) * 8]], axis=0
                ).astype(BF16)
                send_minor(f, t)

        @pl.when(jnp.logical_and(t >= 1, t < steps_all + 1))
        def _():
            a = t - 1
            for f in range(FLOWS):
                d = sense(f)
                block = gath.at[f, a, major(f), turn(minor(f), d)]
                arrived(block, ag_recv.at[1, f, a])
                remote(block, block, send.at[8], ag_recv.at[2, f, a], along_minor(f, -d)).start()

        @pl.when(jnp.logical_and(t >= 2, t < steps_all + 2))
        def _():
            a = t - 2
            for f in range(FLOWS):
                d = sense(f)
                u, v = major(f), minor(f)
                arrived(gath.at[f, a, u, turn(v, -d)], ag_recv.at[0, f, a])
                arrived(gath.at[f, a, u, turn(v, 2)], ag_recv.at[2, f, a])
                block = gath.at[f, a, u]
                remote(block, block, send.at[10], ag_recv.at[4, f, a], along_major(f, -d)).start()
                remote(block, block, send.at[9], ag_recv.at[3, f, a], along_major(f, d)).start()

        @pl.when(t == 2)
        def _():
            for f in range(FLOWS):
                y_out(f, 0)

        @pl.when(jnp.logical_and(t >= 3, t < steps_all + 3))
        def _():
            a = t - 3
            for f in range(FLOWS):
                d = sense(f)
                block = gath.at[f, a, turn(major(f), d)]
                arrived(block, ag_recv.at[4, f, a])
                remote(block, block, send.at[11], ag_recv.at[5, f, a], along_major(f, -d)).start()

        @pl.when(t == 3)
        def _():
            for f in range(FLOWS):
                y_out(f, 1)
            for f in range(FLOWS):
                y_relay(f, 0)

        @pl.when(t >= 4)
        def _():
            a = t - 4
            for f in range(FLOWS):
                d = sense(f)
                u = major(f)
                arrived(gath.at[f, a, turn(u, -d)], ag_recv.at[3, f, a])
                arrived(gath.at[f, a, turn(u, 2)], ag_recv.at[5, f, a])

        @pl.when(t == 4)
        def _():
            for f in range(FLOWS):
                y_out(f, 2)
                y_out(f, 3)
            for f in range(FLOWS):
                y_relay(f, 1)

        @pl.when(t == 5)
        def _():
            for f in range(FLOWS):
                y_relay(f, 2)

        @pl.when(t == 6)
        def _():
            for f in range(FLOWS):
                y_relay(f, 3)

        @pl.when(t >= 5)
        def _():
            s = t - 5
            for f in range(FLOWS):
                product = jnp.dot(perm[f % 2], gath[f, t - 4].reshape(256, strip), preferred_element_type=F32)
                out[s, :, f * strip : (f + 1) * strip] = (0.25 * product).astype(BF16)
            cols = pl.ds(pl.multiple_of(s * width, width), width)
            pltpu.make_async_copy(out.at[s], update_hbm.at[0, :, cols], out_sem.at[2, s]).start()

    stores = [
        pltpu.make_async_copy(first, new_first_hbm.at[0], out_sem.at[0, 0]),
        pltpu.make_async_copy(second, new_second_hbm.at[0], out_sem.at[1, 0]),
    ]
    for store in stores:
        store.start()
    for f in range(FLOWS):
        for k in range(RING):
            arrived(gpart.at[f, y_place(f, k)], gpart_recv.at[f, k])
        mine, theirs = gath[f, 0].reshape(256, strip), gpart[f].reshape(256, strip)
        for j in range(2):
            product = jnp.dot(yperm[f % 2, 0, j], mine, preferred_element_type=F32)
            product = product + jnp.dot(yperm[f % 2, 1, j], theirs, preferred_element_type=F32)
            yout[f, :, j * strip : (j + 1) * strip] = (0.25 * product).astype(BF16)
        store = pltpu.make_async_copy(
            yout.at[f], update_hbm.at[0, :, base + f * pair : base + (f + 1) * pair], out_sem.at[1, 1 + f]
        )
        store.start()
        stores.append(store)
    for k in range(len(plane)):
        arrived(acc, near_send.at[k])
    for k in range(len(column)):
        arrived(acc2, far_send.at[k])
    for k in (0, 1, 2, 9, 10, 11):
        arrived(ra, send.at[k])
    for k in (3, 4, 5, 6, 7, 8):
        arrived(ra2, send.at[k])
    for k in range(2):
        arrived(yrecv, ysem.at[k])
    for k in range(4):
        arrived(ypart, pass_send.at[k])
    for s in range(plain):
        pltpu.make_async_copy(out.at[s], update_hbm.at[0, :, s * width : (s + 1) * width], out_sem.at[2, s]).wait()
    for store in stores:
        store.wait()


def fused(step_count, acts, cotangent, basis, first, second, total_entries):
    _, tokens, ff = cotangent.shape
    depth, rank = basis.shape[1:]
    plain = 5
    strip = ff // (FLOWS * (plain + 2))
    width = FLOWS * strip
    chunks = 4
    out_rows = depth // (2 * RING * RING)
    any_space = pl.BlockSpec(memory_space=pl.ANY)
    limit = 0.25 * total_entries**0.5
    dma = pltpu.SemaphoreType.DMA
    vmem = pltpu.VMEM
    steps_all = plain + 1
    big = vmem((FLOWS, steps_all, 64, strip), BF16)
    small = vmem((FLOWS, steps_all, 16, strip), BF16)
    yshape = (plain, 32, strip)
    half = vmem((FLOWS, RING, 64, strip), BF16)
    return pl.pallas_call(
        functools.partial(step_kernel, plain, strip, limit),
        out_shape=(
            jax.ShapeDtypeStruct((1, out_rows, ff), BF16),
            jax.ShapeDtypeStruct(first.shape, F32),
            jax.ShapeDtypeStruct(second.shape, F32),
        ),
        in_specs=[
            pl.BlockSpec(memory_space=pltpu.SMEM),
            any_space, any_space, any_space, any_space, any_space,
        ],
        out_specs=(any_space, any_space, any_space),
        scratch_shapes=[
            vmem((chunks, tokens, depth // chunks), BF16),
            vmem((depth, rank), BF16),
            vmem((tokens, rank), F32),
            vmem((rank, tokens), BF16),
            vmem((3, tokens, width), BF16),
            vmem((tokens, 2 * width), BF16),
            vmem((FLOWS, steps_all, RING, 64, strip), BF16),
            big, big, big, big,
            vmem((FLOWS, steps_all, RING, 16, strip), BF16),
            small, small, small, small,
            vmem(yshape, BF16),
            vmem(yshape, BF16),
            vmem(yshape, F32),
            vmem((FLOWS, 2, RING, 64, strip), BF16),
            half,
            half,
            vmem((FLOWS, 16, strip), F32),
            vmem((8, ff), F32),
            vmem((8, ff), F32),
            vmem((2, out_rows, rank), BF16),
            vmem((2, 2, 2, out_rows, rank), BF16),
            vmem((FLOWS, steps_all, RING, RING, 16, strip), BF16),
            vmem(yshape, BF16),
            vmem(yshape, BF16),
            vmem((FLOWS, RING, RING, 16, strip), BF16),
            vmem((FLOWS, RING, RING, 16, strip), BF16),
            vmem((plain, out_rows, width), BF16),
            vmem((FLOWS, out_rows, 2 * strip), BF16),
            vmem((8, 128), F32),
            vmem((15, 8, 128), F32),
            vmem((8, 128), F32),
            vmem((7, 8, 128), F32),
            dma((6, FLOWS, steps_all)),
            dma((plain,)),
            dma((6, FLOWS, steps_all)),
            dma((plain,)),
            dma((12,)),
            dma((2,)),
            dma((FLOWS,)),
            dma((FLOWS,)),
            dma((FLOWS, RING)),
            dma((FLOWS, RING)),
            dma((4,)),
            dma((3,)),
            dma,
            dma((2 + 2 * chunks,)),
            dma((15,)),
            dma((15,)),
            dma((7,)),
            dma((7,)),
            dma((3, max(plain, 1 + FLOWS))),
        ],
        compiler_params=pltpu.CompilerParams(
            collective_id=0, has_side_effects=True, vmem_limit_bytes=63 * 1024 * 1024
        ),
        name="galore_step",
    )(step_count, acts, cotangent, basis, first, second)


def make_local(total_entries):
    def local(acts, cotangent, basis, first_moment, second_moment, step_count):
        return fused(step_count, acts, cotangent, basis, first_moment, second_moment, total_entries)

    return local


def solution(mesh, total_entries=4 * 256 * 14336):
    split = Mesh(mesh.devices.reshape(4, 2, 4, 2, 2), AXES)
    return jax.shard_map(
        make_local(total_entries),
        mesh=split,
        in_specs=(
            P(EXPERT, DP, None),
            P(EXPERT, DP, None),
            P(EXPERT, None, None),
            P(EXPERT, DP, None),
            P(EXPERT, DP, None),
            P(),
        ),
        out_specs=(P(EXPERT, DP, None), P(EXPERT, DP, None), P(EXPERT, DP, None)),
        check_vma=False,
    )
```

time: 130 us -> 117 us (0.900)
  Pallas kernels: 118 us -> 110 us
  matrix products: 4.83 us -> 0 us
    pallas_call x1, Pallas kernels: 118 us -> 110 us  [fused(): pl.pallas_call(functools.partial(step_kernel, plain, strip, limit), out_s...]
    dot_general x1 -> x0, matrix products: 4.83 us -> none  [local(): jnp.einsum('td,dr->rt', acts[0], basis[0], preferred_element_type=F32)]
where the time goes in v3:
time: 117 us
  Pallas kernels  110 us (94%)
  local copies, waits for them, and re-layouts  5.82 us (5%)
  between operations  1.3 us (1%)
    pallas_call x1, Pallas kernels, fused(): pl.pallas_call(functools.partial(step_kernel, plain, strip, limit), out_s...  110 us
    unnamed x7, local copies, waits for them, and re-layouts  5.82 us

profile of v3, /device:TPU:0, one launch (start us, length us, event | category | flops | bytes accessed | tf_op | source)
XLA Modules:
  0.0 116.7 jit_solution(12008868868039191088)
XLA Ops:
  1.3 109.6 %galore_step.1 = (bf16[1,128,14336]{2,1,0:T(8,128)(2,1)}, f32[1,8,14336]{2,1,0:T(8,128)}, f32[1,8,14336]{2,1,0:T(8,128)}) custom-call(s32[1]{0:T(128)S(6)} %copy.12.step_ref, bf16[1,512,4096]{2,1,0:T(8,128)(2,1)} %acts_hbm.1, bf16[1,512,14336]{2,1,0:T(8,128)(2,1)} %cot_hbm.1, bf16[1,4096,256]{2,1,0:T(8,128)(2,1)} %basis_hbm.1, f32[1,8,14336]{2,1,0:T(8,128)} %first_hbm.1, ...), custom_call_target="tpu_custom_call" | custom-call | tf_op jit(solution)/shard_map/galore_step/pallas_call | solution.py:508
  110.9 0.0 copy-start.1
  110.9 0.0 copy-start
  110.9 4.3 %copy.13 = bf16[1,128,14336]{2,1,0:T(8,128)(2,1)} copy(bf16[1,128,14336]{2,1,0:T(8,128)(2,1)} %get-tuple-element.6) | data formatting | bytes 7340032
  115.2 0.0 copy-done.1
  115.2 0.8 copy.14
  115.9 0.0 copy-done
  115.9 0.8 copy.15
Async XLA Ops:
  110.9 4.3 %copy-start.1 = (f32[1,8,14336]{2,1,0:T(8,128)S(1)}, f32[1,8,14336]{2,1,0:T(8,128)}, u32[]{:S(2)}) copy-start(f32[1,8,14336]{2,1,0:T(8,128)} %get-tuple-element.7) | copy-start | bytes 1376260
  110.9 5.1 %copy-start = (f32[1,8,14336]{2,1,0:T(8,128)S(1)}, f32[1,8,14336]{2,1,0:T(8,128)}, u32[]{:S(2)}) copy-start(f32[1,8,14336]{2,1,0:T(8,128)} %get-tuple-element.8) | copy-start | bytes 1376260

commit v4 on v3

--- a/solution.py
+++ b/solution.py
@@ -29,13 +29,13 @@
 def step_kernel(
     plain, strip, limit,
     step_ref, acts_hbm, cot_hbm, basis_hbm, first_hbm, second_hbm,
-    update_hbm, new_first_hbm, new_second_hbm,
+    out, new_first, new_second,
     acts, basis, total_acc, reduced, cot, ycot,
     own, ra, rb, rc, mix, own2, ra2, rb2, rc2, mix2, ysend, yrecv, sums,
-    yown, ypass, ypart, ysums, first, second, perm, yperm, gath, nsend, nrecv, gpass, gpart, out, yout,
+    yown, ypass, ypart, ysums, perm, yperm, gath, nsend, nrecv, gpass, gpart,
     acc, near, acc2, far,
     rs_recv, rsy_recv, ag_recv, agy_recv, send, ysem, pass_recv, part_recv, gpass_recv, gpart_recv, pass_send,
-    cot_sem, ycot_sem, in_sem, near_sem, near_send, far_sem, far_send, out_sem,
+    cot_sem, ycot_sem, in_sem, near_sem, near_send, far_sem, far_send,
 ):
     z, h, x = lax.axis_index("dp_0"), lax.axis_index("dp_1"), lax.axis_index("dp_2")
     lo, core = lax.axis_index("expert_0"), lax.axis_index("expert_1")
@@ -44,6 +44,7 @@
     base = plain * width
     steps_all = plain + 1
     nrow = out.shape[1]
+    first, second = new_first.at[0], new_second.at[0]
     dp_index = z * (2 * RING) + h * RING + x
 
     def turn(p, k):
@@ -110,9 +111,9 @@
     for one, two in first_loads:
         two.start()
         one.start()
-    cot_copy(0).start()
     ycot_copy = pltpu.make_async_copy(cot_hbm.at[0, :, base : base + FLOWS * pair], ycot, ycot_sem)
     ycot_copy.start()
+    cot_copy(0).start()
     cot_copy(1).start()
     loads = [
         pltpu.make_async_copy(first_hbm.at[0], first, in_sem.at[0]),
@@ -138,8 +139,26 @@
         remote(own.at[f, t, turn(p, 2)], rb.at[f, t], send.at[1], rs_recv.at[1, f, t], along_major(f, -d)).start()
         remote(own.at[f, t, turn(p, d)], ra.at[f, t], send.at[0], rs_recv.at[0, f, t], along_major(f, d)).start()
 
-    @pl.loop(0, plain + 5)
+    @pl.loop(0, plain + 4)
     def _(t):
+        def y_units(flows):
+            for f in flows:
+                part = jnp.dot(reduced[...], ycot[:, f * pair : (f + 1) * pair], preferred_element_type=F32)
+                for u in range(RING):
+                    for v in range(RING):
+                        zz, xx = (u, v) if f % 2 == 0 else (v, u)
+                        for y in range(2):
+                            r0 = zz * 64 + y * 32 + xx * 8
+                            yown[f, y, u, v * 16 : (v + 1) * 16, :] = jnp.concatenate(
+                                [part[r0 : r0 + 8, :strip], part[r0 : r0 + 8, strip:]], axis=0
+                            ).astype(BF16)
+                remote(yown.at[f, 1 - h], ypass.at[f], pass_send.at[0], pass_recv.at[f], along_y(f)).start()
+
+        @pl.when(t == 0)
+        def _():
+            ycot_copy.wait()
+            y_units((0, 2))
+
         @pl.when(t < plain)
         def _():
             @pl.when(jnp.logical_and(t >= 1, t + 1 < plain))
@@ -160,21 +179,6 @@
                         ).astype(BF16)
                 send_major(f, t)
 
-        @pl.when(t == 0)
-        def _():
-            ycot_copy.wait()
-            for f in (0, 2, 1, 3):
-                part = jnp.dot(reduced[...], ycot[:, f * pair : (f + 1) * pair], preferred_element_type=F32)
-                for u in range(RING):
-                    for v in range(RING):
-                        zz, xx = (u, v) if f % 2 == 0 else (v, u)
-                        for y in range(2):
-                            r0 = zz * 64 + y * 32 + xx * 8
-                            yown[f, y, u, v * 16 : (v + 1) * 16, :] = jnp.concatenate(
-                                [part[r0 : r0 + 8, :strip], part[r0 : r0 + 8, strip:]], axis=0
-                            ).astype(BF16)
-                remote(yown.at[f, 1 - h], ypass.at[f], pass_send.at[0], pass_recv.at[f], along_y(f)).start()
-
         @pl.when(t == plain)
         def _():
             for f in range(FLOWS):
@@ -205,14 +209,49 @@
                 whole = own[f, s, major(f)].astype(F32) + ra[f, s].astype(F32) + rc[f, s].astype(F32)
                 for v in range(RING):
                     own2[f, s, v] = whole[v * 16 : (v + 1) * 16].astype(BF16)
-                remote(
-                    own2.at[f, s, turn(q, 2)], rb2.at[f, s], send.at[4], rs_recv.at[4, f, s], along_minor(f, -d)
-                ).start()
+
+                @pl.when(s == plain)
+                def _():
+                    for k, away in ((5, 2), (4, -d)):
+                        dst = (rb2 if k == 4 else rc2).at[f, plain]
+                        remote(
+                            own2.at[f, plain, turn(q, away)], dst, send.at[k], rs_recv.at[k, f, plain], along_minor(f, away)
+                        ).start()
+
+                @pl.when(s < plain)
+                def _():
+                    remote(
+                        own2.at[f, s, turn(q, 2)], rb2.at[f, s], send.at[4], rs_recv.at[4, f, s], along_minor(f, -d)
+                    ).start()
+
                 remote(
                     own2.at[f, s, turn(q, d)], ra2.at[f, s], send.at[3], rs_recv.at[3, f, s], along_minor(f, d)
                 ).start()
 
-        for turn_of, flows in ((1, (0, 2)), (2, (1, 3))):
+        @pl.when(t == 1)
+        def _():
+            y_units((1, 3))
+
+        @pl.when(t == 3)
+        def _():
+            rows = basis[pl.ds(pl.multiple_of(dp_index * nrow, nrow), nrow), :]
+            r = lax.broadcasted_iota(jnp.int32, (256, 256), 0)
+            q = lax.broadcasted_iota(jnp.int32, (256, 256), 1)
+            for o in range(2):
+                u, v = q // 64, (q // 16) % 4
+                zz, xx = (u, v) if o == 0 else (v, u)
+                place = zz * 64 + xx * 8 + q % 8
+                half = (q // 8) % 2
+                one = jnp.where(place + 32 * half == r, 1.0, 0.0).astype(BF16)
+                perm[o] = jnp.dot(rows, one, preferred_element_type=F32).astype(BF16)
+                for away in range(2):
+                    y = lax.rem(h + away, 2)
+                    for j in range(2):
+                        hit = jnp.logical_and(place + 32 * y == r, half == j)
+                        one = jnp.where(hit, 1.0, 0.0).astype(BF16)
+                        yperm[o, away, j] = jnp.dot(rows, one, preferred_element_type=F32).astype(BF16)
+
+        for turn_of, flows in ((2, (0, 2)), (3, (1, 3))):
 
             @pl.when(t == turn_of)
             def _():
@@ -220,7 +259,7 @@
                     arrived(ypass.at[f], pass_recv.at[f])
                     remote(ypass.at[f], ypart.at[f], pass_send.at[1], part_recv.at[f], along_y(f)).start()
 
-        @pl.when(jnp.logical_and(t >= 3, t < steps_all + 3))
+        @pl.when(jnp.logical_and(t >= 3, t < plain + 3))
         def _():
             s = t - 3
             for f in range(FLOWS):
@@ -243,14 +282,6 @@
                 for j in range(strip // 128):
                     piece = piece + square[i * 8 : (i + 1) * 8, j * 128 : (j + 1) * 128]
             acc[...] = piece
-
-        @pl.when(jnp.logical_and(t >= 5, t < plain + 5))
-        def _():
-            s = t - 5
-            arrived(yrecv.at[s], rsy_recv.at[s])
-            grad = sums[s] + yrecv[s].astype(F32)
-            sums[s] = grad
-            add_squares(grad)
 
         @pl.when(jnp.logical_and(t >= 4, t < plain + 4))
         def _():
@@ -264,35 +295,41 @@
                     held = other
                 else:
                     ysend[s, (f - 1) * 8 : (f + 1) * 8, :] = jnp.concatenate([held, other], axis=0).astype(BF16)
+
+        def y_send(s):
             remote(ysend.at[s], yrecv.at[s], ysem.at[0], rsy_recv.at[s], partner).start()
 
-        @pl.when(t == plain + 4)
-        def _():
-            for f in range(FLOWS):
-                whole = last_two(f, plain)
+        def y_take(s):
+            arrived(yrecv.at[s], rsy_recv.at[s])
+            grad = sums[s] + yrecv[s].astype(F32)
+            sums[s] = grad
+            add_squares(grad)
+
+        @pl.when(t == plain + 1)
+        def _():
+            for s in range(plain - 2):
+                y_send(s)
+
+        @pl.when(t == plain + 2)
+        def _():
+            y_send(plain - 2)
+
+        @pl.when(t == plain + 3)
+        def _():
+            y_send(plain - 1)
+            for s in range(plain - 1):
+                y_take(s)
+            for f in range(FLOWS):
+                arrived(rb2.at[f, plain], rs_recv.at[4, f, plain])
+                whole = last_two(f, plain) + rb2[f, plain].astype(F32)
                 ysums[f] = whole
                 add_squares(whole)
+            y_take(plain - 1)
 
     for k, dev in enumerate(plane):
         remote(acc, near.at[k], near_send.at[k], near_sem.at[k], dev).start()
     for load in loads:
         load.wait()
-    rows = basis[pl.ds(pl.multiple_of(dp_index * nrow, nrow), nrow), :]
-    r = lax.broadcasted_iota(jnp.int32, (256, 256), 0)
-    q = lax.broadcasted_iota(jnp.int32, (256, 256), 1)
-    for o in range(2):
-        u, v = q // 64, (q // 16) % 4
-        zz, xx = (u, v) if o == 0 else (v, u)
-        place = zz * 64 + xx * 8 + q % 8
-        half = (q // 8) % 2
-        one = jnp.where(place + 32 * half == r, 1.0, 0.0).astype(BF16)
-        perm[o] = jnp.dot(rows, one, preferred_element_type=F32).astype(BF16)
-        for away in range(2):
-            y = lax.rem(h + away, 2)
-            for j in range(2):
-                hit = jnp.logical_and(place + 32 * y == r, half == j)
-                one = jnp.where(hit, 1.0, 0.0).astype(BF16)
-                yperm[o, away, j] = jnp.dot(rows, one, preferred_element_type=F32).astype(BF16)
     steps = jnp.full((8, 128), step_ref[0], jnp.int32)
     corr_one = 1.0 - powers(0.9, steps)
     corr_two = 1.0 - powers(0.999, steps)
@@ -345,7 +382,28 @@
         top = adam(pl.ds(base + f * pair, strip), ysums[f, :8])
         bottom = adam(pl.ds(base + f * pair + strip, strip), ysums[f, 8:])
         gath[f, 0, major(f), minor(f)] = jnp.concatenate([top, bottom], axis=0).astype(BF16)
-        send_minor(f, 0)
+        d = sense(f)
+        block = gath.at[f, 0, major(f), minor(f)]
+        for k, away in ((2, 2), (1, -d), (0, d)):
+            remote(block, block, send.at[6 + k], ag_recv.at[k, f, 0], along_minor(f, away)).start()
+
+    def send_block(f, a):
+        d = sense(f)
+        block = gath.at[f, a, major(f)]
+        remote(block, block, send.at[10], ag_recv.at[4, f, a], along_major(f, -d)).start()
+        remote(block, block, send.at[9], ag_recv.at[3, f, a], along_major(f, d)).start()
+
+    def relay_block(f, a):
+        d = sense(f)
+        block = gath.at[f, a, turn(major(f), d)]
+        arrived(block, ag_recv.at[4, f, a])
+        remote(block, block, send.at[11], ag_recv.at[5, f, a], along_major(f, -d)).start()
+
+    def take_block(f, a):
+        d = sense(f)
+        u = major(f)
+        arrived(gath.at[f, a, turn(u, -d)], ag_recv.at[3, f, a])
+        arrived(gath.at[f, a, turn(u, 2)], ag_recv.at[5, f, a])
 
     @pl.loop(0, plain + 5)
     def _(t):
@@ -373,7 +431,23 @@
                 ).astype(BF16)
                 send_minor(f, t)
 
-        @pl.when(jnp.logical_and(t >= 1, t < steps_all + 1))
+        @pl.when(t == 1)
+        def _():
+            for f in range(FLOWS):
+                for k, away in ((0, -sense(f)), (1, sense(f)), (2, 2)):
+                    arrived(gath.at[f, 0, major(f), turn(minor(f), away)], ag_recv.at[k, f, 0])
+                send_block(f, 0)
+            for f in range(FLOWS):
+                y_out(f, 0)
+
+        @pl.when(t == 2)
+        def _():
+            for f in range(FLOWS):
+                relay_block(f, 0)
+            for f in range(FLOWS):
+                y_out(f, 1)
+
+        @pl.when(jnp.logical_and(t >= 2, t < steps_all + 1))
         def _():
             a = t - 1
             for f in range(FLOWS):
@@ -382,7 +456,7 @@
                 arrived(block, ag_recv.at[1, f, a])
                 remote(block, block, send.at[8], ag_recv.at[2, f, a], along_minor(f, -d)).start()
 
-        @pl.when(jnp.logical_and(t >= 2, t < steps_all + 2))
+        @pl.when(jnp.logical_and(t >= 3, t < steps_all + 2))
         def _():
             a = t - 2
             for f in range(FLOWS):
@@ -390,56 +464,35 @@
                 u, v = major(f), minor(f)
                 arrived(gath.at[f, a, u, turn(v, -d)], ag_recv.at[0, f, a])
                 arrived(gath.at[f, a, u, turn(v, 2)], ag_recv.at[2, f, a])
-                block = gath.at[f, a, u]
-                remote(block, block, send.at[10], ag_recv.at[4, f, a], along_major(f, -d)).start()
-                remote(block, block, send.at[9], ag_recv.at[3, f, a], along_major(f, d)).start()
-
-        @pl.when(t == 2)
-        def _():
-            for f in range(FLOWS):
-                y_out(f, 0)
-
-        @pl.when(jnp.logical_and(t >= 3, t < steps_all + 3))
-        def _():
-            a = t - 3
-            for f in range(FLOWS):
-                d = sense(f)
-                block = gath.at[f, a, turn(major(f), d)]
-                arrived(block, ag_recv.at[4, f, a])
-                remote(block, block, send.at[11], ag_recv.at[5, f, a], along_major(f, -d)).start()
+                send_block(f, a)
+
+        @pl.when(jnp.logical_and(t >= 4, t < steps_all + 3))
+        def _():
+            for f in range(FLOWS):
+                relay_block(f, t - 3)
 
         @pl.when(t == 3)
         def _():
             for f in range(FLOWS):
-                y_out(f, 1)
-            for f in range(FLOWS):
-                y_relay(f, 0)
-
-        @pl.when(t >= 4)
-        def _():
-            a = t - 4
-            for f in range(FLOWS):
-                d = sense(f)
-                u = major(f)
-                arrived(gath.at[f, a, turn(u, -d)], ag_recv.at[3, f, a])
-                arrived(gath.at[f, a, turn(u, 2)], ag_recv.at[5, f, a])
-
-        @pl.when(t == 4)
-        def _():
-            for f in range(FLOWS):
+                take_block(f, 0)
                 y_out(f, 2)
                 y_out(f, 3)
-            for f in range(FLOWS):
+
+        @pl.when(t >= 5)
+        def _():
+            for f in range(FLOWS):
+                take_block(f, t - 4)
+
+        @pl.when(t == 5)
+        def _():
+            for f in range(FLOWS):
+                y_relay(f, 0)
                 y_relay(f, 1)
 
-        @pl.when(t == 5)
+        @pl.when(t == 6)
         def _():
             for f in range(FLOWS):
                 y_relay(f, 2)
-
-        @pl.when(t == 6)
-        def _():
-            for f in range(FLOWS):
                 y_relay(f, 3)
 
         @pl.when(t >= 5)
@@ -447,16 +500,8 @@
             s = t - 5
             for f in range(FLOWS):
                 product = jnp.dot(perm[f % 2], gath[f, t - 4].reshape(256, strip), preferred_element_type=F32)
-                out[s, :, f * strip : (f + 1) * strip] = (0.25 * product).astype(BF16)
-            cols = pl.ds(pl.multiple_of(s * width, width), width)
-            pltpu.make_async_copy(out.at[s], update_hbm.at[0, :, cols], out_sem.at[2, s]).start()
-
-    stores = [
-        pltpu.make_async_copy(first, new_first_hbm.at[0], out_sem.at[0, 0]),
-        pltpu.make_async_copy(second, new_second_hbm.at[0], out_sem.at[1, 0]),
-    ]
-    for store in stores:
-        store.start()
+                cols = pl.ds(pl.multiple_of(s * width + f * strip, strip), strip)
+                out[0, :, cols] = (0.25 * product).astype(BF16)
     for f in range(FLOWS):
         for k in range(RING):
             arrived(gpart.at[f, y_place(f, k)], gpart_recv.at[f, k])
@@ -464,12 +509,8 @@
         for j in range(2):
             product = jnp.dot(yperm[f % 2, 0, j], mine, preferred_element_type=F32)
             product = product + jnp.dot(yperm[f % 2, 1, j], theirs, preferred_element_type=F32)
-            yout[f, :, j * strip : (j + 1) * strip] = (0.25 * product).astype(BF16)
-        store = pltpu.make_async_copy(
-            yout.at[f], update_hbm.at[0, :, base + f * pair : base + (f + 1) * pair], out_sem.at[1, 1 + f]
-        )
-        store.start()
-        stores.append(store)
+            start = base + f * pair + j * strip
+            out[0, :, start : start + strip] = (0.25 * product).astype(BF16)
     for k in range(len(plane)):
         arrived(acc, near_send.at[k])
     for k in range(len(column)):
@@ -482,10 +523,6 @@
         arrived(yrecv, ysem.at[k])
     for k in range(4):
         arrived(ypart, pass_send.at[k])
-    for s in range(plain):
-        pltpu.make_async_copy(out.at[s], update_hbm.at[0, :, s * width : (s + 1) * width], out_sem.at[2, s]).wait()
-    for store in stores:
-        store.wait()
 
 
 def fused(step_count, acts, cotangent, basis, first, second, total_entries):
@@ -497,6 +534,7 @@
     chunks = 4
     out_rows = depth // (2 * RING * RING)
     any_space = pl.BlockSpec(memory_space=pl.ANY)
+    in_vmem = pl.BlockSpec(memory_space=pltpu.VMEM)
     limit = 0.25 * total_entries**0.5
     dma = pltpu.SemaphoreType.DMA
     vmem = pltpu.VMEM
@@ -508,15 +546,15 @@
     return pl.pallas_call(
         functools.partial(step_kernel, plain, strip, limit),
         out_shape=(
-            jax.ShapeDtypeStruct((1, out_rows, ff), BF16),
-            jax.ShapeDtypeStruct(first.shape, F32),
-            jax.ShapeDtypeStruct(second.shape, F32),
+            vmem((1, out_rows, ff), BF16),
+            vmem((1, 8, ff), F32),
+            vmem((1, 8, ff), F32),
         ),
         in_specs=[
             pl.BlockSpec(memory_space=pltpu.SMEM),
             any_space, any_space, any_space, any_space, any_space,
         ],
-        out_specs=(any_space, any_space, any_space),
+        out_specs=(in_vmem,) * 3,
         scratch_shapes=[
             vmem((chunks, tokens, depth // chunks), BF16),
             vmem((depth, rank), BF16),
@@ -535,8 +573,6 @@
             half,
             half,
             vmem((FLOWS, 16, strip), F32),
-            vmem((8, ff), F32),
-            vmem((8, ff), F32),
             vmem((2, out_rows, rank), BF16),
             vmem((2, 2, 2, out_rows, rank), BF16),
             vmem((FLOWS, steps_all, RING, RING, 16, strip), BF16),
@@ -544,8 +580,6 @@
             vmem(yshape, BF16),
             vmem((FLOWS, RING, RING, 16, strip), BF16),
             vmem((FLOWS, RING, RING, 16, strip), BF16),
-            vmem((plain, out_rows, width), BF16),
-            vmem((FLOWS, out_rows, 2 * strip), BF16),
             vmem((8, 128), F32),
             vmem((15, 8, 128), F32),
             vmem((8, 128), F32),
@@ -568,10 +602,9 @@
             dma((15,)),
             dma((7,)),
             dma((7,)),
-            dma((3, max(plain, 1 + FLOWS))),
         ],
         compiler_params=pltpu.CompilerParams(
-            collective_id=0, has_side_effects=True, vmem_limit_bytes=63 * 1024 * 1024
+            collective_id=0, has_side_effects=True, vmem_limit_bytes=56 * 1024 * 1024
         ),
         name="galore_step",
     )(step_count, acts, cotangent, basis, first, second)

time: 117 us -> 111 us (0.949)
  Pallas kernels: 110 us -> 106 us
  local copies, waits for them, and re-layouts: 5.82 us -> 3.37 us
    pallas_call x1, Pallas kernels: 110 us -> 106 us  [fused(): pl.pallas_call(functools.partial(step_kernel, plain, strip, limit), out_s...]
    unnamed x7 -> x3, local copies, waits for them, and re-layouts: 5.82 us -> 3.37 us
where the time goes in v4:
time: 111 us
  Pallas kernels  106 us (95%)
  local copies, waits for them, and re-layouts  3.37 us (3%)
  between operations  1.29 us (1%)
    pallas_call x1, Pallas kernels, fused(): pl.pallas_call(functools.partial(step_kernel, plain, strip, limit), out_s...  106 us
    unnamed x3, local copies, waits for them, and re-layouts  3.37 us

profile of v4, /device:TPU:0, one launch (start us, length us, event | category | flops | bytes accessed | tf_op | source)
XLA Modules:
  0.0 111.0 jit_solution(13388653534090837346)
XLA Ops:
  1.3 106.4 %galore_step.1 = (bf16[1,128,14336]{2,1,0:T(8,128)(2,1)S(1)}, f32[1,8,14336]{2,1,0:T(8,128)S(1)}, f32[1,8,14336]{2,1,0:T(8,128)S(1)}) custom-call(s32[1]{0:T(128)S(6)} %copy.15.step_ref, bf16[1,512,4096]{2,1,0:T(8,128)(2,1)} %acts_hbm.1, bf16[1,512,14336]{2,1,0:T(8,128)(2,1)} %cot_hbm.1, bf16[1,4096,256]{2,1,0:T(8,128)(2,1)} %basis_hbm.1, ...), custom_call_target="tpu_custom_call" | custom-call | tf_op jit(solution)/shard_map/galore_step/pallas_call | solution.py:546
  107.7 1.8 %copy.12 = bf16[1,128,14336]{2,1,0:T(8,128)(2,1)} copy(bf16[1,128,14336]{2,1,0:T(8,128)(2,1)S(1)} %get-tuple-element.3) | data formatting | bytes 7340032
  109.5 0.8 copy.13
  110.3 0.8 copy.14

commit v5 on v4

--- a/solution.py
+++ b/solution.py
@@ -157,7 +157,7 @@
         @pl.when(t == 0)
         def _():
             ycot_copy.wait()
-            y_units((0, 2))
+            y_units((0, 3))
 
         @pl.when(t < plain)
         def _():
@@ -181,11 +181,19 @@
 
         @pl.when(t == plain)
         def _():
-            for f in range(FLOWS):
+            for f in (0, 3, 1, 2):
                 arrived(ypart.at[f], part_recv.at[f])
                 for u in range(RING):
                     own[f, plain, u] = (yown[f, h, u].astype(F32) + ypart[f, u].astype(F32)).astype(BF16)
                 send_major(f, plain)
+
+        for turn_of, flows in ((2, (0, 3)), (3, (1, 2))):
+
+            @pl.when(t == turn_of)
+            def _():
+                for f in flows:
+                    arrived(ypass.at[f], pass_recv.at[f])
+                    remote(ypass.at[f], ypart.at[f], pass_send.at[1], part_recv.at[f], along_y(f)).start()
 
         @pl.when(jnp.logical_and(t >= 1, t < steps_all + 1))
         def _():
@@ -230,7 +238,7 @@
 
         @pl.when(t == 1)
         def _():
-            y_units((1, 3))
+            y_units((1, 2))
 
         @pl.when(t == 3)
         def _():
@@ -250,14 +258,6 @@
                         hit = jnp.logical_and(place + 32 * y == r, half == j)
                         one = jnp.where(hit, 1.0, 0.0).astype(BF16)
                         yperm[o, away, j] = jnp.dot(rows, one, preferred_element_type=F32).astype(BF16)
-
-        for turn_of, flows in ((2, (0, 2)), (3, (1, 3))):
-
-            @pl.when(t == turn_of)
-            def _():
-                for f in flows:
-                    arrived(ypass.at[f], pass_recv.at[f])
-                    remote(ypass.at[f], ypart.at[f], pass_send.at[1], part_recv.at[f], along_y(f)).start()
 
         @pl.when(jnp.logical_and(t >= 3, t < plain + 3))
         def _():
@@ -502,15 +502,19 @@
                 product = jnp.dot(perm[f % 2], gath[f, t - 4].reshape(256, strip), preferred_element_type=F32)
                 cols = pl.ds(pl.multiple_of(s * width + f * strip, strip), strip)
                 out[0, :, cols] = (0.25 * product).astype(BF16)
-    for f in range(FLOWS):
-        for k in range(RING):
-            arrived(gpart.at[f, y_place(f, k)], gpart_recv.at[f, k])
-        mine, theirs = gath[f, 0].reshape(256, strip), gpart[f].reshape(256, strip)
-        for j in range(2):
-            product = jnp.dot(yperm[f % 2, 0, j], mine, preferred_element_type=F32)
-            product = product + jnp.dot(yperm[f % 2, 1, j], theirs, preferred_element_type=F32)
-            start = base + f * pair + j * strip
-            out[0, :, start : start + strip] = (0.25 * product).astype(BF16)
+
+        @pl.when(t == plain + 3)
+        def _():
+            for f in range(FLOWS):
+                for k in range(RING):
+                    arrived(gpart.at[f, y_place(f, k)], gpart_recv.at[f, k])
+                mine, theirs = gath[f, 0].reshape(256, strip), gpart[f].reshape(256, strip)
+                for j in range(2):
+                    product = jnp.dot(yperm[f % 2, 0, j], mine, preferred_element_type=F32)
+                    product = product + jnp.dot(yperm[f % 2, 1, j], theirs, preferred_element_type=F32)
+                    start = base + f * pair + j * strip
+                    out[0, :, start : start + strip] = (0.25 * product).astype(BF16)
+
     for k in range(len(plane)):
         arrived(acc, near_send.at[k])
     for k in range(len(column)):

time: 111 us -> 109 us (0.982)
  Pallas kernels: 106 us -> 104 us
    pallas_call x1, Pallas kernels: 106 us -> 104 us  [fused(): pl.pallas_call(functools.partial(step_kernel, plain, strip, limit), out_s...]
where the time goes in v5:
time: 109 us
  Pallas kernels  104 us (95%)
  local copies, waits for them, and re-layouts  3.37 us (3%)
  between operations  1.29 us (1%)
    pallas_call x1, Pallas kernels, fused(): pl.pallas_call(functools.partial(step_kernel, plain, strip, limit), out_s...  104 us
    unnamed x3, local copies, waits for them, and re-layouts  3.37 us

profile of v5, /device:TPU:0, one launch (start us, length us, event | category | flops | bytes accessed | tf_op | source)
XLA Modules:
  0.0 109.1 jit_solution(18199884583417433530)
XLA Ops:
  1.3 104.5 %galore_step.1 = (bf16[1,128,14336]{2,1,0:T(8,128)(2,1)S(1)}, f32[1,8,14336]{2,1,0:T(8,128)S(1)}, f32[1,8,14336]{2,1,0:T(8,128)S(1)}) custom-call(s32[1]{0:T(128)S(6)} %copy.15.step_ref, bf16[1,512,4096]{2,1,0:T(8,128)(2,1)} %acts_hbm.1, bf16[1,512,14336]{2,1,0:T(8,128)(2,1)} %cot_hbm.1, bf16[1,4096,256]{2,1,0:T(8,128)(2,1)} %basis_hbm.1, ...), custom_call_target="tpu_custom_call" | custom-call | tf_op jit(solution)/shard_map/galore_step/pallas_call | solution.py:550
  105.8 1.8 %copy.12 = bf16[1,128,14336]{2,1,0:T(8,128)(2,1)} copy(bf16[1,128,14336]{2,1,0:T(8,128)(2,1)S(1)} %get-tuple-element.3) | data formatting | bytes 7340032
  107.6 0.8 copy.13
  108.4 0.8 copy.14

commit v6 on v5

--- a/solution.py
+++ b/solution.py
@@ -218,15 +218,15 @@
                 for v in range(RING):
                     own2[f, s, v] = whole[v * 16 : (v + 1) * 16].astype(BF16)
 
-                @pl.when(s == plain)
+                @pl.when(s >= plain - 1)
                 def _():
                     for k, away in ((5, 2), (4, -d)):
-                        dst = (rb2 if k == 4 else rc2).at[f, plain]
+                        dst = (rb2 if k == 4 else rc2).at[f, s]
                         remote(
-                            own2.at[f, plain, turn(q, away)], dst, send.at[k], rs_recv.at[k, f, plain], along_minor(f, away)
+                            own2.at[f, s, turn(q, away)], dst, send.at[k], rs_recv.at[k, f, s], along_minor(f, away)
                         ).start()
 
-                @pl.when(s < plain)
+                @pl.when(s < plain - 1)
                 def _():
                     remote(
                         own2.at[f, s, turn(q, 2)], rb2.at[f, s], send.at[4], rs_recv.at[4, f, s], along_minor(f, -d)
@@ -259,7 +259,7 @@
                         one = jnp.where(hit, 1.0, 0.0).astype(BF16)
                         yperm[o, away, j] = jnp.dot(rows, one, preferred_element_type=F32).astype(BF16)
 
-        @pl.when(jnp.logical_and(t >= 3, t < plain + 3))
+        @pl.when(jnp.logical_and(t >= 3, t < plain + 2))
         def _():
             s = t - 3
             for f in range(FLOWS):
@@ -283,11 +283,13 @@
                     piece = piece + square[i * 8 : (i + 1) * 8, j * 128 : (j + 1) * 128]
             acc[...] = piece
 
-        @pl.when(jnp.logical_and(t >= 4, t < plain + 4))
-        def _():
-            s = t - 4
-            for f in range(FLOWS):
-                whole = last_two(f, s)
+        def last_three(f, s):
+            arrived(rb2.at[f, s], rs_recv.at[4, f, s])
+            return last_two(f, s) + rb2[f, s].astype(F32)
+
+        def split_rows(s, take):
+            for f in range(FLOWS):
+                whole = take(f, s)
                 low = h == 0
                 sums[s, f * 8 : (f + 1) * 8, :] = jnp.where(low, whole[:8], whole[8:])
                 other = jnp.where(low, whole[8:], whole[:8])
@@ -296,6 +298,10 @@
                 else:
                     ysend[s, (f - 1) * 8 : (f + 1) * 8, :] = jnp.concatenate([held, other], axis=0).astype(BF16)
 
+        @pl.when(jnp.logical_and(t >= 4, t < plain + 3))
+        def _():
+            split_rows(t - 4, last_two)
+
         def y_send(s):
             remote(ysend.at[s], yrecv.at[s], ysem.at[0], rsy_recv.at[s], partner).start()
 
@@ -313,15 +319,15 @@
         @pl.when(t == plain + 2)
         def _():
             y_send(plain - 2)
+            split_rows(plain - 1, last_three)
+            y_send(plain - 1)
 
         @pl.when(t == plain + 3)
         def _():
-            y_send(plain - 1)
             for s in range(plain - 1):
                 y_take(s)
             for f in range(FLOWS):
-                arrived(rb2.at[f, plain], rs_recv.at[4, f, plain])
-                whole = last_two(f, plain) + rb2[f, plain].astype(F32)
+                whole = last_three(f, plain)
                 ysums[f] = whole
                 add_squares(whole)
             y_take(plain - 1)

time: 109 us -> 107 us (0.982)
  Pallas kernels: 104 us -> 102 us
    pallas_call x1, Pallas kernels: 104 us -> 102 us  [fused(): pl.pallas_call(functools.partial(step_kernel, plain, strip, limit), out_s...]
where the time goes in v6:
time: 107 us
  Pallas kernels  102 us (95%)
  local copies, waits for them, and re-layouts  3.37 us (3%)
  between operations  1.29 us (1%)
    pallas_call x1, Pallas kernels, fused(): pl.pallas_call(functools.partial(step_kernel, plain, strip, limit), out_s...  102 us
    unnamed x3, local copies, waits for them, and re-layouts  3.37 us

profile of v6, /device:TPU:0, one launch (start us, length us, event | category | flops | bytes accessed | tf_op | source)
XLA Modules:
  0.0 106.9 jit_solution(14492797937453904751)
XLA Ops:
  1.3 102.2 %galore_step.1 = (bf16[1,128,14336]{2,1,0:T(8,128)(2,1)S(1)}, f32[1,8,14336]{2,1,0:T(8,128)S(1)}, f32[1,8,14336]{2,1,0:T(8,128)S(1)}) custom-call(s32[1]{0:T(128)S(6)} %copy.15.step_ref, bf16[1,512,4096]{2,1,0:T(8,128)(2,1)} %acts_hbm.1, bf16[1,512,14336]{2,1,0:T(8,128)(2,1)} %cot_hbm.1, bf16[1,4096,256]{2,1,0:T(8,128)(2,1)} %basis_hbm.1, ...), custom_call_target="tpu_custom_call" | custom-call | tf_op jit(solution)/shard_map/galore_step/pallas_call | solution.py:556
  103.5 1.8 %copy.12 = bf16[1,128,14336]{2,1,0:T(8,128)(2,1)} copy(bf16[1,128,14336]{2,1,0:T(8,128)(2,1)S(1)} %get-tuple-element.3) | data formatting | bytes 7340032
  105.3 0.8 copy.13
  106.1 0.8 copy.14
